TPU v7x, 32 devices: a 4x4x1 block of a 4x4x8 slice. The times are simulated.
32 devices in a mesh: rep: 1 (over z), dp: 32 (over y, x, core).
Axes of the slice: x: 4, y: 4, z: 1, core: 2. Of those that a mesh axis runs over, the one named last changes fastest.
The devices are a block of a 4x4x8 slice.
Arguments:
- audio_x: bfloat16 [32, 1500, 384], P(('rep', 'dp'))
- attn_w: bfloat16 [2, 4, 384, 384], P(None, None, None, 'dp')
- fc1_w: bfloat16 [2, 384, 1536], P(None, None, 'dp')
- fc2_w: bfloat16 [2, 1536, 384], P(None, 'dp')
- vec_d: bfloat16 [2, 8, 384], P(None, None, 'dp')
- b1_vec: bfloat16 [2, 1536], P(None, 'dp')
Outputs:
- output: bfloat16 [32, 1500, 384], P(('rep', 'dp'))
All inputs are finite; a program needn't handle non-finite values.
Results may differ from a plain program's by a relative error of at most 0.0135751.
Values are sent between devices in bfloat16 or wider.
A program may use at most 768 MiB of HBM per device.

v0:
```python
import functools
import math

import jax
import jax.numpy as jnp
from jax import lax
from jax.experimental import pallas as pl
from jax.experimental.pallas import tpu as pltpu
from jax.sharding import PartitionSpec as P

HEAD_DIM = 64
LN_EPSILON = 1e-5
LANES = 128
TILE = 512
F32, BF16 = jnp.float32, jnp.bfloat16
NT = (((1,), (1,)), ((), ()))


def mm(a, b):
    return jnp.dot(a, b, preferred_element_type=F32)


def mm_nt(a, b):
    return lax.dot_general(a, b, NT, preferred_element_type=F32)


def eye(n):
    row = lax.broadcasted_iota(jnp.int32, (n, n), 0)
    col = lax.broadcasted_iota(jnp.int32, (n, n), 1)
    return (row == col).astype(F32).astype(BF16)


def kernel(n, x_ref, w_ref, out_ref, g_ref, wa_ref, w2t_ref, h_ref, a_ref, q_ref, k_ref, v_ref, o_ref, z_ref,
           s0_ref, s1_ref, m0_ref, m1_ref, send_sem, recv_sem, fsend_sem, frecv_sem):
    layers, rows, width = w_ref.shape
    _, frames, model = x_ref.shape
    aug = wa_ref.shape[2]
    heads = model // HEAD_DIM
    pairs = heads // 2
    hidden = z_ref.shape[0]
    tiles = h_ref.shape[0]
    keys = s0_ref.shape[0]
    side = math.isqrt(n // 2)
    chips = n // 2

    me = lax.axis_index("dp")
    core = lax.rem(me, 2)
    chip = me // 2
    partner = me + 1 - 2 * core

    def peer(k, sign):
        dy, dx = divmod(k, side)
        y = lax.rem(chip // side + sign * dy + side, side)
        x = lax.rem(lax.rem(chip, side) + sign * dx + side, side)
        return 2 * (y * side + x) + core

    barrier = pltpu.get_barrier_semaphore()
    for k in range(chips):
        pl.semaphore_signal(barrier, inc=1, device_id={"dp": peer(k, 1) if k else partner})
    pl.semaphore_wait(barrier, chips)

    pieces = []
    for layer in range(layers):
        pieces += [(layer, 0, aug), (layer, aug, width - aug)]

    def slot(ref, piece, dev):
        layer, lo, size = pieces[piece]
        return ref.at[layer, pl.ds(pl.multiple_of(dev * rows, 16), rows), pl.ds(lo, size)]

    def send(piece, k):
        layer, lo, size = pieces[piece]
        return pltpu.make_async_remote_copy(
            src_ref=w_ref.at[layer, :, pl.ds(lo, size)], dst_ref=slot(g_ref, piece, me),
            send_sem=send_sem.at[piece, k], recv_sem=recv_sem.at[piece, k],
            device_id={"dp": peer(k, 1) if k else partner})

    def forward(piece, k):
        src = peer(k, -1)
        return pltpu.make_async_remote_copy(
            src_ref=slot(g_ref, piece, src), dst_ref=slot(g_ref, piece, src),
            send_sem=fsend_sem.at[piece, k - 1], recv_sem=frecv_sem.at[piece, k - 1],
            device_id={"dp": partner})

    def start_forward(piece):
        for k in range(1, chips):
            send(piece, k).wait_recv()
            forward(piece, k).start()

    def wait_piece(piece):
        send(piece, 0).wait_recv()
        for k in range(1, chips):
            forward(piece, k).wait_recv()

    for piece in range(len(pieces)):
        for k in range(chips):
            send(piece, k).start()

    own = pl.ds(pl.multiple_of(me * rows, 16), rows)
    for layer in range(layers):
        g_ref[layer, own, :] = w_ref[layer]
    ones_row = (lax.broadcasted_iota(jnp.int32, (aug - model, TILE), 0) == 0).astype(F32).astype(BF16)
    for t in range(tiles):
        a_ref[t, model:, :] = ones_row
        o_ref[t, model:, :] = ones_row
    zero_half = jnp.zeros((HEAD_DIM, TILE), BF16)
    for h in range(heads):
        other = HEAD_DIM * (1 - h % 2)
        for t in range(tiles):
            q_ref[h, t, other:other + HEAD_DIM, :] = zero_half
        extra = v_ref.shape[1] - HEAD_DIM
        v_ref[h, HEAD_DIM:, :] = (lax.broadcasted_iota(jnp.int32, (extra, v_ref.shape[2]), 0) == 0).astype(F32).astype(BF16)
    eye_m = eye(model)
    h_ref[tiles - 1, :, :] = jnp.zeros((model, TILE), BF16)
    for t in range(tiles):
        size = min(TILE, frames - t * TILE)
        h_ref[t, :, 0:size] = mm_nt(eye_m, x_ref[0, t * TILE:t * TILE + size, :]).astype(BF16)

    def layer_norm(z, gain, shift):
        mean = jnp.sum(z, axis=0, keepdims=True) * (1.0 / model)
        c = z - mean
        var = jnp.sum(c * c, axis=0, keepdims=True) * (1.0 / model)
        return (c * lax.rsqrt(var + LN_EPSILON) * gain + shift).astype(BF16)

    def column(j, lane):
        return wa_ref[j, :, lane:lane + 1].astype(F32)

    def unpack(layer):
        block = 4 * HEAD_DIM
        row = lax.broadcasted_iota(jnp.int32, (block, block), 0)
        col = lax.broadcasted_iota(jnp.int32, (block, block), 1)
        perm = (col == lax.rem(row, HEAD_DIM) * 4 + row // HEAD_DIM).astype(F32).astype(BF16)
        for h in range(heads):
            mixed = mm(perm, g_ref[layer, h * block:(h + 1) * block, 0:aug]).astype(BF16)
            for j in range(4):
                wa_ref[j, h * HEAD_DIM:(h + 1) * HEAD_DIM, :] = mixed[j * HEAD_DIM:(j + 1) * HEAD_DIM]

    scale = HEAD_DIM ** -0.25
    eye_k = eye(TILE // 2)

    def pre(t):
        lanes = pl.ds(pl.multiple_of(t * TILE, TILE), TILE)
        a_ref[t, 0:model, :] = layer_norm(h_ref[t].astype(F32), column(0, model + 1), column(1, model + 1))
        a = a_ref[t]
        q = (mm(wa_ref[0], a) * scale).astype(BF16)
        for h in range(heads):
            half = HEAD_DIM * (h % 2)
            q_ref[h, t, half:half + HEAD_DIM, :] = q[h * HEAD_DIM:(h + 1) * HEAD_DIM]
        kt = (mm(wa_ref[1], a) * scale).astype(BF16)
        half = TILE // 2
        for b in range(2):
            kn = mm_nt(eye_k, kt[:, b * half:(b + 1) * half]).astype(BF16)
            for p in range(pairs):
                k_ref[p, pl.ds(pl.multiple_of(t * TILE + b * half, half), half), :] = kn[:, p * LANES:(p + 1) * LANES]
        v = mm(wa_ref[2], a).astype(BF16)
        for h in range(heads):
            v_ref[h, 0:HEAD_DIM, lanes] = v[h * HEAD_DIM:(h + 1) * HEAD_DIM]

    s_refs, m_refs = (s0_ref, s1_ref), (m0_ref, m1_ref)

    def scores(p, hh, t, buf):
        s = mm(k_ref[p, 0:keys, :], q_ref[2 * p + hh, t])
        last = keys - 8
        row = lax.broadcasted_iota(jnp.int32, (8, TILE), 0) + last
        tail = jnp.where(row < frames, s[last:], -jnp.inf)
        s_refs[buf][0:last, :] = s[0:last]
        s_refs[buf][last:, :] = tail
        m_refs[buf][...] = jnp.maximum(jnp.max(s[0:last], axis=0, keepdims=True), jnp.max(tail, axis=0, keepdims=True))

    def values(p, hh, t, buf):
        h = 2 * p + hh
        e = jnp.exp(s_refs[buf][...] - m_refs[buf][...]).astype(BF16)
        o = mm(v_ref[h, :, 0:keys], e)
        inv = 1.0 / o[HEAD_DIM:HEAD_DIM + 1]
        o_ref[t, pl.ds(pl.multiple_of(h * HEAD_DIM, HEAD_DIM), HEAD_DIM), :] = (o[0:HEAD_DIM] * inv).astype(BF16)

    def attention(events):
        steps = [(hh, t) for hh in range(2) for t in range(tiles)]

        def body(p, carry):
            for at, event in events.items():
                pl.when(p == at)(event)
            for j, (hh, t) in enumerate(steps):
                scores(p, hh, t, j % 2)
                if j:
                    values(p, *steps[j - 1], (j - 1) % 2)
                else:
                    values(jnp.maximum(p - 1, 0), *steps[-1], 1)
            return carry

        lax.fori_loop(0, pairs, body, 0)
        values(pairs - 1, *steps[-1], 1)

    def unpack_mlp(layer):
        for b in range(hidden // TILE):
            w2 = g_ref[layer, b * TILE:(b + 1) * TILE, 2 * aug:2 * aug + model]
            w2t_ref[:, b * TILE:(b + 1) * TILE] = mm_nt(eye_m, w2).astype(BF16)

    def post(layer, t):
        r = h_ref[t].astype(F32) + mm(wa_ref[3], o_ref[t])
        r = r.astype(BF16)
        a_ref[t, 0:model, :] = layer_norm(r.astype(F32), column(2, model + 1), column(3, model + 1))
        c = a_ref[t]
        step = 2 * LANES
        for b in range(hidden // step):
            u = mm(g_ref[layer, b * step:(b + 1) * step, aug:2 * aug], c)
            z_ref[b * step:(b + 1) * step, :] = (0.5 * u * (1.0 + lax.erf(u * (2.0 ** -0.5)))).astype(BF16)
        y = r.astype(F32) + (mm(w2t_ref[...], z_ref[...]) + column(0, model + 2))
        h_ref[t] = y.astype(BF16)

    for layer in range(layers):
        piece = 2 * layer
        if layer == 0:
            start_forward(piece)
        wait_piece(piece)
        unpack(layer)
        lax.fori_loop(0, tiles, lambda t, c: (pre(t), c)[1], 0)
        attention({pairs - 1: functools.partial(start_forward, piece + 1)})
        if layer + 1 < layers:
            start_forward(piece + 2)
        wait_piece(piece + 1)
        unpack_mlp(layer)
        lax.fori_loop(0, tiles, lambda t, c, layer=layer: (post(layer, t), c)[1], 0)

    for t in range(tiles):
        for b in range(2):
            lo = t * TILE + b * (TILE // 2)
            size = min(TILE // 2, frames - lo)
            y = mm_nt(eye_k, h_ref[t, :, b * (TILE // 2):(b + 1) * (TILE // 2)]).astype(BF16)
            out_ref[0, lo:lo + size, :] = y[0:size]

    for piece in range(len(pieces)):
        for k in range(chips):
            send(piece, k).wait_send()
        for k in range(1, chips):
            forward(piece, k).wait_send()


def solution(mesh):
    n = mesh.shape["dp"]

    def body(audio_x, attn_w, fc1_w, fc2_w, vec_d, b1_vec):
        layers, four, model, cols = attn_w.shape
        hidden_cols = fc1_w.shape[2]
        batch, frames, _ = audio_x.shape
        hidden = hidden_cols * n
        aug = model + LANES
        rows = four * cols
        vec = jnp.moveaxis(vec_d, 1, 2)
        bias = jnp.stack([vec[..., 0], jnp.zeros_like(vec[..., 0]), vec[..., 1], vec[..., 2]], -1)
        b2 = jnp.pad(vec[..., 3:4], ((0, 0), (0, 0), (0, four - 1)))
        extra = jnp.stack([bias, vec[..., 4:8], b2], -1)
        extra = jnp.pad(extra, ((0, 0), (0, 0), (0, 0), (0, LANES - extra.shape[-1])))
        attn = jnp.concatenate([jnp.transpose(attn_w, (0, 3, 1, 2)), extra], -1).reshape(layers, rows, aug)
        b1 = jnp.pad(b1_vec[..., None], ((0, 0), (0, 0), (0, LANES - 1)))
        packed = jnp.concatenate([attn, jnp.transpose(fc1_w, (0, 2, 1)), b1, fc2_w], -1)

        tiles = -(-frames // TILE)
        padded = tiles * TILE
        keys = -(-frames // 16) * 16
        heads = model // HEAD_DIM
        chips = n // 2
        pieces = 2 * layers
        vmem = pl.BlockSpec(memory_space=pltpu.VMEM)
        return pl.pallas_call(
            functools.partial(kernel, n),
            out_shape=jax.ShapeDtypeStruct(audio_x.shape, audio_x.dtype),
            in_specs=[vmem, vmem],
            out_specs=vmem,
            scratch_shapes=[
                pltpu.VMEM((layers, n * rows, packed.shape[-1]), BF16),
                pltpu.VMEM((four, model, aug), BF16),
                pltpu.VMEM((model, hidden), BF16),
                pltpu.VMEM((tiles, model, TILE), BF16),
                pltpu.VMEM((tiles, aug, TILE), BF16),
                pltpu.VMEM((heads, tiles, LANES, TILE), BF16),
                pltpu.VMEM((heads // 2, padded, LANES), BF16),
                pltpu.VMEM((heads, HEAD_DIM + 16, padded), BF16),
                pltpu.VMEM((tiles, aug, TILE), BF16),
                pltpu.VMEM((hidden, TILE), BF16),
                pltpu.VMEM((keys, TILE), F32),
                pltpu.VMEM((keys, TILE), F32),
                pltpu.VMEM((1, TILE), F32),
                pltpu.VMEM((1, TILE), F32),
                pltpu.SemaphoreType.DMA((pieces, chips)),
                pltpu.SemaphoreType.DMA((pieces, chips)),
                pltpu.SemaphoreType.DMA((pieces, chips - 1)),
                pltpu.SemaphoreType.DMA((pieces, chips - 1)),
            ],
            compiler_params=pltpu.CompilerParams(
                collective_id=0, has_side_effects=True, vmem_limit_bytes=60 * 1024 * 1024),
        )(audio_x, packed)

    return jax.shard_map(
        body, mesh=mesh,
        in_specs=(P(('rep', 'dp')), P(None, None, None, 'dp'), P(None, None, 'dp'), P(None, 'dp', None), P(None, None, 'dp'), P(None, 'dp')),
        out_specs=P(('rep', 'dp')), check_vma=False)
```

profile of v0, /device:TPU:98, one launch (start us, length us, event | category | flops | bytes accessed | tf_op | source)
XLA Modules:
  0.0 98.3 jit_solution(12162069590605424132)
XLA Ops:
  0.0 0.1 pad.25.clone
  0.1 0.7 slice.19
  0.8 0.7 slice_bitcast_fusion
  1.5 0.8 fusion.6
  2.2 0.1 maximum_bitcast_fusion
  2.3 0.2 copy.9
  2.5 0.8 copy.8
  3.2 0.9 fusion.5
  4.2 1.6 %fusion.3.w_ref = bf16[2,48,1408]{2,1,0:T(8,128)(2,1)} fusion(bf16[2,48,1]{2,1,0:T(8,128)(2,1)S(1)} %copy.8, bf16[2,48,384]{2,1,0:T(8,128)(2,1)} %param.9, bf16[2,48,384]{2,1,0:T(8,128)(2,1)} %bitcast.12, bf16[2,48,512]{2,1,0:T(8,128)(2,1)S(1)} %reshape.3), kind=kLoop, calls=%fused_computation.5 | loop fusion | flops 1622016 | bytes 516288 | tf_op jit(solution)/shard_map/concatenate | solution.py:255
  5.9 90.1 %shard_map.64 = bf16[1,1500,384]{2,1,0:T(8,128)(2,1)} custom-call(bf16[1,1500,384]{2,1,0:T(8,128)(2,1)} %x_ref.1, bf16[2,48,1408]{2,1,0:T(8,128)(2,1)} %fusion.3.w_ref), custom_call_target="tpu_custom_call" | custom-call | tf_op jit(solution)/shard_map/pallas_call | solution.py:264
  95.9 2.4 %copy.11 = bf16[1,1500,384]{2,1,0:T(8,128)(2,1)} copy(bf16[1,1500,384]{2,1,0:T(8,128)(2,1)} %shard_map.64) | data formatting | bytes 2304000
  (2 shorter events, 0.0 us)
where the time goes:
time: 98.7 us; the launch traced here: 98.3 us
  Pallas kernels  90.1 us (91%)
  local copies, waits for them, and re-layouts  5.55 us (6%)
  other arithmetic  2.67 us (3%)
    pallas_call x1, Pallas kernels, body(): pl.pallas_call(functools.partial(kernel, n), out_shape=jax.ShapeDtypeStru...  90.1 us
    unnamed x2, local copies, waits for them, and re-layouts  2.53 us

commit v1 on v0

--- a/solution.py
+++ b/solution.py
@@ -1,5 +1,4 @@
 import functools
-import math
 
 import jax
 import jax.numpy as jnp
@@ -30,70 +29,139 @@
     return (row == col).astype(F32).astype(BF16)
 
 
-def kernel(n, x_ref, w_ref, out_ref, g_ref, wa_ref, w2t_ref, h_ref, a_ref, q_ref, k_ref, v_ref, o_ref, z_ref,
-           s0_ref, s1_ref, m0_ref, m1_ref, send_sem, recv_sem, fsend_sem, frecv_sem):
+RING = 4
+
+
+def relay_plan():
+    messages, complete = [], {}
+
+    def add(*message):
+        messages.append(message)
+        return len(messages) - 1
+
+    for half in range(2):
+        d1, d2 = half, 1 - half
+
+        def at(a, b):
+            offset = [0, 0]
+            offset[d1], offset[d2] = a % RING, b % RING
+            return tuple(offset)
+
+        both = (1, -1)
+        part = {1: 0, -1: 1}
+        own = {(d, s): add(1, half, None, at(0, 0), d, s, ()) for d in (d1, d2) for s in both}
+        far = {s: add(2, half, part[s], at(-s, 0), d1, s, (own[d1, s],)) for s in both}
+        side = {(s, r): add(2, half, None, at(-s, 0), d2, r, (own[d1, s],)) for s in both for r in both}
+        col = {r: add(2, half, part[r], at(0, -r), d2, r, (own[d2, r],)) for r in both}
+        turn = {r: add(3, half, None, at(2, 0), d2, r, (far[1], far[-1])) for r in both}
+        diag = {(s, r): add(3, half, part[r], at(-s, -r), d2, r, (side[s, r],)) for s in both for r in both}
+        last = {r: add(4, half, part[r], at(2, -r), d2, r, (turn[r],)) for r in both}
+        for s in both:
+            complete[half, at(-s, 0)] = (own[d1, s],)
+            complete[half, at(0, -s)] = (own[d2, s],)
+            complete[half, at(2, -s)] = (turn[s],)
+            complete[half, at(-s, 2)] = (diag[s, 1], diag[s, -1])
+            for r in both:
+                complete[half, at(-s, -r)] = (side[s, r],)
+        complete[half, at(2, 0)] = (far[1], far[-1])
+        complete[half, at(0, 2)] = (col[1], col[-1])
+        complete[half, at(2, 2)] = (last[1], last[-1])
+    return messages, complete
+
+
+MESSAGES, COMPLETE = relay_plan()
+BLOCKS = list(COMPLETE)
+
+
+class Planner:
+    def __init__(self):
+        self.arrived, self.passed = set(), set()
+
+    def step(self, piece, step):
+        actions = []
+        for m, message in enumerate(MESSAGES):
+            if message[0] == step:
+                actions += self.need(piece, message[-1])
+                actions.append(("start", piece, m))
+        if step == 1:
+            actions.append(("pass", piece, len(BLOCKS)))
+        return actions + self.hand_over(piece)
+
+    def need(self, piece, deps):
+        actions = [("wait", piece, m) for m in deps if (piece, m) not in self.arrived]
+        self.arrived.update((piece, m) for m in deps)
+        return actions
+
+    def hand_over(self, piece, everything=False):
+        actions = []
+        for b, block in enumerate(BLOCKS):
+            if (piece, b) in self.passed:
+                continue
+            if everything:
+                actions += self.need(piece, COMPLETE[block])
+            if all((piece, m) in self.arrived for m in COMPLETE[block]):
+                actions.append(("pass", piece, b))
+                self.passed.add((piece, b))
+        if everything:
+            actions += self.need(piece, range(len(MESSAGES)))
+        return actions
+
+
+def kernel(n, x_hbm, attn_ref, fc1_ref, fc2_ref, vec_ref, b1_ref, out_ref, w_ref, g_ref, wa_ref, w2t_ref, x_ref, h_ref, a_ref,
+           q_ref, k_ref, v_ref, o_ref, z_ref, s0_ref, s1_ref, m0_ref, m1_ref, x_sem, send_sem, recv_sem, fsend_sem, frecv_sem):
     layers, rows, width = w_ref.shape
-    _, frames, model = x_ref.shape
+    frames, model = x_ref.shape
     aug = wa_ref.shape[2]
     heads = model // HEAD_DIM
     pairs = heads // 2
     hidden = z_ref.shape[0]
     tiles = h_ref.shape[0]
     keys = s0_ref.shape[0]
-    side = math.isqrt(n // 2)
-    chips = n // 2
+
+    fetch_x = pltpu.make_async_copy(x_hbm.at[0], x_ref, x_sem)
+    fetch_x.start()
 
     me = lax.axis_index("dp")
     core = lax.rem(me, 2)
     chip = me // 2
+    chip_x, chip_y = lax.rem(chip, RING), chip // RING
+
+    def device(offset):
+        x = lax.rem(chip_x + offset[0] + RING, RING)
+        y = lax.rem(chip_y + offset[1] + RING, RING)
+        return 2 * (y * RING + x) + core
+
     partner = me + 1 - 2 * core
-
-    def peer(k, sign):
-        dy, dx = divmod(k, side)
-        y = lax.rem(chip // side + sign * dy + side, side)
-        x = lax.rem(lax.rem(chip, side) + sign * dx + side, side)
-        return 2 * (y * side + x) + core
+    neighbour = {(d, s): device((s, 0) if d == 0 else (0, s)) for d in range(2) for s in (1, -1)}
 
     barrier = pltpu.get_barrier_semaphore()
-    for k in range(chips):
-        pl.semaphore_signal(barrier, inc=1, device_id={"dp": peer(k, 1) if k else partner})
-    pl.semaphore_wait(barrier, chips)
-
-    pieces = []
+    for dev in [*neighbour.values(), partner]:
+        pl.semaphore_signal(barrier, inc=1, device_id={"dp": dev})
+
+    def pick(layer, want):
+        row = lax.broadcasted_iota(jnp.int32, (rows, vec_ref.shape[1]), 0)
+        col = lax.broadcasted_iota(jnp.int32, (rows, vec_ref.shape[1]), 1)
+        sel = jnp.zeros(row.shape, F32)
+        for j, r in enumerate(want):
+            if r is not None:
+                sel = jnp.where((lax.rem(row, 4) == j) & (col == r), 1.0, sel)
+        spread = mm(sel, vec_ref[layer].astype(F32))
+        row = lax.broadcasted_iota(jnp.int32, spread.shape, 0)
+        col = lax.broadcasted_iota(jnp.int32, spread.shape, 1)
+        return jnp.sum(jnp.where(row // 4 == col, spread, 0.0), axis=1, keepdims=True)
+
+    lane = lax.broadcasted_iota(jnp.int32, (rows, LANES), 1)
     for layer in range(layers):
-        pieces += [(layer, 0, aug), (layer, aug, width - aug)]
-
-    def slot(ref, piece, dev):
-        layer, lo, size = pieces[piece]
-        return ref.at[layer, pl.ds(pl.multiple_of(dev * rows, 16), rows), pl.ds(lo, size)]
-
-    def send(piece, k):
-        layer, lo, size = pieces[piece]
-        return pltpu.make_async_remote_copy(
-            src_ref=w_ref.at[layer, :, pl.ds(lo, size)], dst_ref=slot(g_ref, piece, me),
-            send_sem=send_sem.at[piece, k], recv_sem=recv_sem.at[piece, k],
-            device_id={"dp": peer(k, 1) if k else partner})
-
-    def forward(piece, k):
-        src = peer(k, -1)
-        return pltpu.make_async_remote_copy(
-            src_ref=slot(g_ref, piece, src), dst_ref=slot(g_ref, piece, src),
-            send_sem=fsend_sem.at[piece, k - 1], recv_sem=frecv_sem.at[piece, k - 1],
-            device_id={"dp": partner})
-
-    def start_forward(piece):
-        for k in range(1, chips):
-            send(piece, k).wait_recv()
-            forward(piece, k).start()
-
-    def wait_piece(piece):
-        send(piece, 0).wait_recv()
-        for k in range(1, chips):
-            forward(piece, k).wait_recv()
-
-    for piece in range(len(pieces)):
-        for k in range(chips):
-            send(piece, k).start()
+        w_ref[layer, :, 0:model] = attn_ref[layer]
+        entry = [pick(layer, want) for want in ((0, None, 1, 2), (4, 5, 6, 7), (3, None, None, None))]
+        extra = jnp.where(lane == 0, entry[0], jnp.where(lane == 1, entry[1], jnp.where(lane == 2, entry[2], 0.0)))
+        w_ref[layer, :, model:aug] = extra.astype(BF16)
+        w_ref[layer, :, aug:aug + model] = fc1_ref[layer]
+        row = lax.broadcasted_iota(jnp.int32, (rows, rows), 0)
+        col = lax.broadcasted_iota(jnp.int32, (rows, rows), 1)
+        b1 = jnp.sum(jnp.where(row == col, b1_ref[layer:layer + 1, :].astype(F32), 0.0), axis=1, keepdims=True)
+        w_ref[layer, :, aug + model:2 * aug] = jnp.where(lane == 0, b1, 0.0).astype(BF16)
+        w_ref[layer, :, 2 * aug:width] = fc2_ref[layer]
 
     own = pl.ds(pl.multiple_of(me * rows, 16), rows)
     for layer in range(layers):
@@ -102,6 +170,61 @@
     for t in range(tiles):
         a_ref[t, model:, :] = ones_row
         o_ref[t, model:, :] = ones_row
+
+    pl.semaphore_wait(barrier, len(neighbour) + 1)
+
+    pieces = [(0, 0, aug), (0, aug, width - aug)] + [(layer, 0, width) for layer in range(1, layers)]
+
+    def lanes_of(piece, half, quarter):
+        _, lo, size = pieces[piece]
+        units = size // LANES
+        first = -(-units // 2)
+        lo, units = (lo, first) if half == 0 else (lo + first * LANES, units - first)
+        first = -(-units // 2)
+        if quarter is not None:
+            lo, units = (lo, first) if quarter == 0 else (lo + first * LANES, units - first)
+        return pl.ds(lo, units * LANES)
+
+    def slot(piece, dev, lanes):
+        return g_ref.at[pieces[piece][0], pl.ds(pl.multiple_of(dev * rows, 16), rows), lanes]
+
+    def relay(piece, m):
+        step, half, quarter, offset, d, s, _ = MESSAGES[m]
+        lanes = lanes_of(piece, half, quarter)
+        dst = slot(piece, device(offset), lanes)
+        src = w_ref.at[pieces[piece][0], :, lanes] if step == 1 else dst
+        return pltpu.make_async_remote_copy(
+            src_ref=src, dst_ref=dst, send_sem=send_sem.at[piece, m], recv_sem=recv_sem.at[piece, m],
+            device_id={"dp": neighbour[d, s]})
+
+    def hand(piece, b):
+        if b == len(BLOCKS):
+            lanes = pl.ds(*pieces[piece][1:])
+            src, dst = w_ref.at[pieces[piece][0], :, lanes], slot(piece, me, lanes)
+        else:
+            half, offset = BLOCKS[b]
+            src = dst = slot(piece, device(offset), lanes_of(piece, half, None))
+        return pltpu.make_async_remote_copy(
+            src_ref=src, dst_ref=dst, send_sem=fsend_sem.at[piece, b], recv_sem=frecv_sem.at[piece, b],
+            device_id={"dp": partner})
+
+    def run(actions):
+        for kind, piece, index in actions:
+            if kind == "start":
+                relay(piece, index).start()
+            elif kind == "wait":
+                relay(piece, index).wait_recv()
+            else:
+                hand(piece, index).start()
+
+    def finish(piece):
+        run(plan.hand_over(piece, everything=True))
+        for b in range(len(BLOCKS) + 1):
+            hand(piece, b).wait_recv()
+
+    plan = Planner()
+    run(plan.step(0, 1))
+
     zero_half = jnp.zeros((HEAD_DIM, TILE), BF16)
     for h in range(heads):
         other = HEAD_DIM * (1 - h % 2)
@@ -109,11 +232,19 @@
             q_ref[h, t, other:other + HEAD_DIM, :] = zero_half
         extra = v_ref.shape[1] - HEAD_DIM
         v_ref[h, HEAD_DIM:, :] = (lax.broadcasted_iota(jnp.int32, (extra, v_ref.shape[2]), 0) == 0).astype(F32).astype(BF16)
+
+    run(plan.step(0, 2))
+
     eye_m = eye(model)
     h_ref[tiles - 1, :, :] = jnp.zeros((model, TILE), BF16)
+    fetch_x.wait()
     for t in range(tiles):
         size = min(TILE, frames - t * TILE)
-        h_ref[t, :, 0:size] = mm_nt(eye_m, x_ref[0, t * TILE:t * TILE + size, :]).astype(BF16)
+        h_ref[t, :, 0:size] = mm_nt(eye_m, x_ref[t * TILE:t * TILE + size, :]).astype(BF16)
+
+    run(plan.step(0, 3))
+    run(plan.step(0, 4))
+    run(plan.step(1, 1))
 
     def layer_norm(z, gain, shift):
         mean = jnp.sum(z, axis=0, keepdims=True) * (1.0 / model)
@@ -177,9 +308,10 @@
         steps = [(hh, t) for hh in range(2) for t in range(tiles)]
 
         def body(p, carry):
-            for at, event in events.items():
-                pl.when(p == at)(event)
             for j, (hh, t) in enumerate(steps):
+                for (at, when), actions in events.items():
+                    if when == j:
+                        pl.when(p == at)(functools.partial(run, actions))
                 scores(p, hh, t, j % 2)
                 if j:
                     values(p, *steps[j - 1], (j - 1) % 2)
@@ -208,18 +340,36 @@
         h_ref[t] = y.astype(BF16)
 
     for layer in range(layers):
-        piece = 2 * layer
+        more = layer + 1 < layers
         if layer == 0:
-            start_forward(piece)
-        wait_piece(piece)
+            finish(0)
         unpack(layer)
         lax.fori_loop(0, tiles, lambda t, c: (pre(t), c)[1], 0)
-        attention({pairs - 1: functools.partial(start_forward, piece + 1)})
-        if layer + 1 < layers:
-            start_forward(piece + 2)
-        wait_piece(piece + 1)
+        events = {}
+        if layer == 0:
+            run(plan.step(1, 2))
+            events[0, 3] = plan.step(1, 3)
+            events[1, 0] = plan.step(1, 4)
+        if more:
+            events.setdefault((1, 0), []).extend(plan.step(layer + 2, 1))
+            events[1, 3] = plan.step(layer + 2, 2)
+            events[2, 0] = (plan.hand_over(1, everything=True) if layer == 0 else []) + plan.step(layer + 2, 3)
+            events[2, 3] = plan.step(layer + 2, 4)
+        attention(events)
+        if layer == 0:
+            finish(1)
         unpack_mlp(layer)
-        lax.fori_loop(0, tiles, lambda t, c, layer=layer: (post(layer, t), c)[1], 0)
+        late = plan.hand_over(layer + 2, everything=True) if more else []
+
+        def tile(t, carry, layer=layer, late=late):
+            if late:
+                pl.when(t == 1)(functools.partial(run, late))
+            post(layer, t)
+            return carry
+
+        lax.fori_loop(0, tiles, tile, 0)
+        if more:
+            finish(layer + 2)
 
     for t in range(tiles):
         for b in range(2):
@@ -229,10 +379,10 @@
             out_ref[0, lo:lo + size, :] = y[0:size]
 
     for piece in range(len(pieces)):
-        for k in range(chips):
-            send(piece, k).wait_send()
-        for k in range(1, chips):
-            forward(piece, k).wait_send()
+        for m in range(len(MESSAGES)):
+            relay(piece, m).wait_send()
+        for b in range(len(BLOCKS) + 1):
+            hand(piece, b).wait_send()
 
 
 def solution(mesh):
@@ -245,31 +395,26 @@
         hidden = hidden_cols * n
         aug = model + LANES
         rows = four * cols
-        vec = jnp.moveaxis(vec_d, 1, 2)
-        bias = jnp.stack([vec[..., 0], jnp.zeros_like(vec[..., 0]), vec[..., 1], vec[..., 2]], -1)
-        b2 = jnp.pad(vec[..., 3:4], ((0, 0), (0, 0), (0, four - 1)))
-        extra = jnp.stack([bias, vec[..., 4:8], b2], -1)
-        extra = jnp.pad(extra, ((0, 0), (0, 0), (0, 0), (0, LANES - extra.shape[-1])))
-        attn = jnp.concatenate([jnp.transpose(attn_w, (0, 3, 1, 2)), extra], -1).reshape(layers, rows, aug)
-        b1 = jnp.pad(b1_vec[..., None], ((0, 0), (0, 0), (0, LANES - 1)))
-        packed = jnp.concatenate([attn, jnp.transpose(fc1_w, (0, 2, 1)), b1, fc2_w], -1)
+        attn = jnp.transpose(attn_w, (0, 3, 1, 2)).reshape(layers, rows, model)
+        fc1 = jnp.transpose(fc1_w, (0, 2, 1))
 
         tiles = -(-frames // TILE)
         padded = tiles * TILE
         keys = -(-frames // 16) * 16
         heads = model // HEAD_DIM
-        chips = n // 2
-        pieces = 2 * layers
+        pieces = layers + 1
         vmem = pl.BlockSpec(memory_space=pltpu.VMEM)
         return pl.pallas_call(
             functools.partial(kernel, n),
             out_shape=jax.ShapeDtypeStruct(audio_x.shape, audio_x.dtype),
-            in_specs=[vmem, vmem],
+            in_specs=[pl.BlockSpec(memory_space=pl.ANY)] + [vmem] * 5,
             out_specs=vmem,
             scratch_shapes=[
-                pltpu.VMEM((layers, n * rows, packed.shape[-1]), BF16),
+                pltpu.VMEM((layers, rows, 2 * aug + model), BF16),
+                pltpu.VMEM((layers, n * rows, 2 * aug + model), BF16),
                 pltpu.VMEM((four, model, aug), BF16),
                 pltpu.VMEM((model, hidden), BF16),
+                pltpu.VMEM((frames, model), BF16),
                 pltpu.VMEM((tiles, model, TILE), BF16),
                 pltpu.VMEM((tiles, aug, TILE), BF16),
                 pltpu.VMEM((heads, tiles, LANES, TILE), BF16),
@@ -281,14 +426,15 @@
                 pltpu.VMEM((keys, TILE), F32),
                 pltpu.VMEM((1, TILE), F32),
                 pltpu.VMEM((1, TILE), F32),
-                pltpu.SemaphoreType.DMA((pieces, chips)),
-                pltpu.SemaphoreType.DMA((pieces, chips)),
-                pltpu.SemaphoreType.DMA((pieces, chips - 1)),
-                pltpu.SemaphoreType.DMA((pieces, chips - 1)),
+                pltpu.SemaphoreType.DMA,
+                pltpu.SemaphoreType.DMA((pieces, len(MESSAGES))),
+                pltpu.SemaphoreType.DMA((pieces, len(MESSAGES))),
+                pltpu.SemaphoreType.DMA((pieces, len(BLOCKS) + 1)),
+                pltpu.SemaphoreType.DMA((pieces, len(BLOCKS) + 1)),
             ],
             compiler_params=pltpu.CompilerParams(
                 collective_id=0, has_side_effects=True, vmem_limit_bytes=60 * 1024 * 1024),
-        )(audio_x, packed)
+        )(audio_x, attn, fc1, fc2_w, vec_d, b1_vec)
 
     return jax.shard_map(
         body, mesh=mesh,

time: 98.7 us -> 98.7 us (level)
  the two profiles are of different devices: /device:TPU:98 before, /device:TPU:97 now
where the time goes in v1:
time: 98.7 us; the launch traced here: 98.2 us
  Pallas kernels  94.3 us (96%)
  local copies, waits for them, and re-layouts  3.92 us (4%)
    pallas_call x1, Pallas kernels, body(): pl.pallas_call(functools.partial(kernel, n), out_shape=jax.ShapeDtypeStru...  94.3 us
    unnamed x1, local copies, waits for them, and re-layouts  2.38 us

profile of v1, /device:TPU:97, one launch (start us, length us, event | category | flops | bytes accessed | tf_op | source)
XLA Modules:
  0.0 98.2 jit_solution(5660219947855839474)
XLA Ops:
  0.0 1.5 %reshape.3.attn_ref = bf16[2,48,384]{2,1,0:T(8,128)(2,1)} reshape(bf16[2,12,4,384]{3,2,1,0:T(4,128)(2,1)} %bitcast.3) | data formatting | bytes 147456 | tf_op jit(solution)/shard_map/reshape | solution.py:398
  1.5 94.3 %shard_map.64 = bf16[1,1500,384]{2,1,0:T(8,128)(2,1)} custom-call(bf16[1,1500,384]{2,1,0:T(8,128)(2,1)} %x_hbm.1, bf16[2,48,384]{2,1,0:T(8,128)(2,1)} %reshape.3.attn_ref, bf16[2,48,384]{2,1,0:T(8,128)(2,1)} %bitcast.2, bf16[2,48,384]{2,1,0:T(8,128)(2,1)} %fc2_ref.1, bf16[2,8,12]{2,1,0:T(8,128)(2,1)} %vec_ref.1, bf16[2,48]{1,0:T(2,128)(2,1)} %b1_ref.1), custom_call_target="tpu_custom_call" | custom-call | tf_op jit(solution)/shard_map/pallas_call | solution.py:407
  95.8 2.4 %copy.8 = bf16[1,1500,384]{2,1,0:T(8,128)(2,1)} copy(bf16[1,1500,384]{2,1,0:T(8,128)(2,1)} %shard_map.64) | data formatting | bytes 2304000

commit v2 on v1

--- a/solution.py
+++ b/solution.py
@@ -39,33 +39,24 @@
         messages.append(message)
         return len(messages) - 1
 
-    for half in range(2):
-        d1, d2 = half, 1 - half
-
-        def at(a, b):
-            offset = [0, 0]
-            offset[d1], offset[d2] = a % RING, b % RING
-            return tuple(offset)
-
-        both = (1, -1)
-        part = {1: 0, -1: 1}
-        own = {(d, s): add(1, half, None, at(0, 0), d, s, ()) for d in (d1, d2) for s in both}
-        far = {s: add(2, half, part[s], at(-s, 0), d1, s, (own[d1, s],)) for s in both}
-        side = {(s, r): add(2, half, None, at(-s, 0), d2, r, (own[d1, s],)) for s in both for r in both}
-        col = {r: add(2, half, part[r], at(0, -r), d2, r, (own[d2, r],)) for r in both}
-        turn = {r: add(3, half, None, at(2, 0), d2, r, (far[1], far[-1])) for r in both}
-        diag = {(s, r): add(3, half, part[r], at(-s, -r), d2, r, (side[s, r],)) for s in both for r in both}
-        last = {r: add(4, half, part[r], at(2, -r), d2, r, (turn[r],)) for r in both}
-        for s in both:
-            complete[half, at(-s, 0)] = (own[d1, s],)
-            complete[half, at(0, -s)] = (own[d2, s],)
-            complete[half, at(2, -s)] = (turn[s],)
-            complete[half, at(-s, 2)] = (diag[s, 1], diag[s, -1])
-            for r in both:
-                complete[half, at(-s, -r)] = (side[s, r],)
-        complete[half, at(2, 0)] = (far[1], far[-1])
-        complete[half, at(0, 2)] = (col[1], col[-1])
-        complete[half, at(2, 2)] = (last[1], last[-1])
+    def at(a, b):
+        return a % RING, b % RING
+
+    both = (1, -1)
+    axes = [(1, 0), (-1, 0), (0, 1), (0, -1)]
+    corners = [(a, b) for a in both for b in both]
+    own = {to: add(1, (0, 1), at(0, 0), to, ()) for to in axes + corners}
+    for (a, b), m in own.items():
+        complete[at(-a, -b)] = (m,)
+    for part, s in enumerate(both):
+        for r in (0, 1, -1):
+            m = add(2, (part, 2), at(-s, -r), (s, 0), (own[s, r],))
+            complete[at(2, -r)] = complete.get(at(2, -r), ()) + (m,)
+            m = add(2, (part, 2), at(-r, -s), (0, s), (own[r, s],))
+            complete[at(-r, 2)] = complete.get(at(-r, 2), ()) + (m,)
+    for part, (a, b) in enumerate(corners):
+        m = add(2, (part, 4), at(-a, -b), (a, b), (own[a, b],))
+        complete[at(2, 2)] = complete.get(at(2, 2), ()) + (m,)
     return messages, complete
 
 
@@ -107,10 +98,10 @@
         return actions
 
 
-def kernel(n, x_hbm, attn_ref, fc1_ref, fc2_ref, vec_ref, b1_ref, out_ref, w_ref, g_ref, wa_ref, w2t_ref, x_ref, h_ref, a_ref,
-           q_ref, k_ref, v_ref, o_ref, z_ref, s0_ref, s1_ref, m0_ref, m1_ref, x_sem, send_sem, recv_sem, fsend_sem, frecv_sem):
+def kernel(n, x_hbm, attn_ref, fc1_ref, fc2_ref, vec_ref, b1_ref, out_hbm, w_ref, row_ref, g_ref, wa_ref, w2t_ref, x_ref, y_ref, h_ref, a_ref,
+           q_ref, k_ref, v_ref, o_ref, z_ref, s0_ref, s1_ref, m0_ref, m1_ref, x_sem, out_sem, send_sem, recv_sem, fsend_sem, frecv_sem):
     layers, rows, width = w_ref.shape
-    frames, model = x_ref.shape
+    _, frames, model = x_hbm.shape
     aug = wa_ref.shape[2]
     heads = model // HEAD_DIM
     pairs = heads // 2
@@ -132,7 +123,7 @@
         return 2 * (y * RING + x) + core
 
     partner = me + 1 - 2 * core
-    neighbour = {(d, s): device((s, 0) if d == 0 else (0, s)) for d in range(2) for s in (1, -1)}
+    neighbour = {to: device(to) for step, _, _, to, _ in MESSAGES if step == 1}
 
     barrier = pltpu.get_barrier_semaphore()
     for dev in [*neighbour.values(), partner]:
@@ -152,7 +143,9 @@
 
     lane = lax.broadcasted_iota(jnp.int32, (rows, LANES), 1)
     for layer in range(layers):
-        w_ref[layer, :, 0:model] = attn_ref[layer]
+        for c in range(rows // 4):
+            row_ref[4 * c:4 * c + 4, :] = attn_ref[layer, c].astype(F32)
+        w_ref[layer, :, 0:model] = row_ref[...].astype(BF16)
         entry = [pick(layer, want) for want in ((0, None, 1, 2), (4, 5, 6, 7), (3, None, None, None))]
         extra = jnp.where(lane == 0, entry[0], jnp.where(lane == 1, entry[1], jnp.where(lane == 2, entry[2], 0.0)))
         w_ref[layer, :, model:aug] = extra.astype(BF16)
@@ -175,35 +168,30 @@
 
     pieces = [(0, 0, aug), (0, aug, width - aug)] + [(layer, 0, width) for layer in range(1, layers)]
 
-    def lanes_of(piece, half, quarter):
+    def lanes_of(piece, part, parts):
         _, lo, size = pieces[piece]
         units = size // LANES
-        first = -(-units // 2)
-        lo, units = (lo, first) if half == 0 else (lo + first * LANES, units - first)
-        first = -(-units // 2)
-        if quarter is not None:
-            lo, units = (lo, first) if quarter == 0 else (lo + first * LANES, units - first)
-        return pl.ds(lo, units * LANES)
+        first, last = -(-units * part // parts), -(-units * (part + 1) // parts)
+        return pl.ds(lo + first * LANES, (last - first) * LANES)
 
     def slot(piece, dev, lanes):
         return g_ref.at[pieces[piece][0], pl.ds(pl.multiple_of(dev * rows, 16), rows), lanes]
 
     def relay(piece, m):
-        step, half, quarter, offset, d, s, _ = MESSAGES[m]
-        lanes = lanes_of(piece, half, quarter)
+        step, part, offset, to, _ = MESSAGES[m]
+        lanes = lanes_of(piece, *part)
         dst = slot(piece, device(offset), lanes)
         src = w_ref.at[pieces[piece][0], :, lanes] if step == 1 else dst
         return pltpu.make_async_remote_copy(
             src_ref=src, dst_ref=dst, send_sem=send_sem.at[piece, m], recv_sem=recv_sem.at[piece, m],
-            device_id={"dp": neighbour[d, s]})
+            device_id={"dp": neighbour[to]})
 
     def hand(piece, b):
+        lanes = lanes_of(piece, 0, 1)
         if b == len(BLOCKS):
-            lanes = pl.ds(*pieces[piece][1:])
             src, dst = w_ref.at[pieces[piece][0], :, lanes], slot(piece, me, lanes)
         else:
-            half, offset = BLOCKS[b]
-            src = dst = slot(piece, device(offset), lanes_of(piece, half, None))
+            src = dst = slot(piece, device(BLOCKS[b]), lanes)
         return pltpu.make_async_remote_copy(
             src_ref=src, dst_ref=dst, send_sem=fsend_sem.at[piece, b], recv_sem=frecv_sem.at[piece, b],
             device_id={"dp": partner})
@@ -233,8 +221,6 @@
         extra = v_ref.shape[1] - HEAD_DIM
         v_ref[h, HEAD_DIM:, :] = (lax.broadcasted_iota(jnp.int32, (extra, v_ref.shape[2]), 0) == 0).astype(F32).astype(BF16)
 
-    run(plan.step(0, 2))
-
     eye_m = eye(model)
     h_ref[tiles - 1, :, :] = jnp.zeros((model, TILE), BF16)
     fetch_x.wait()
@@ -242,8 +228,7 @@
         size = min(TILE, frames - t * TILE)
         h_ref[t, :, 0:size] = mm_nt(eye_m, x_ref[t * TILE:t * TILE + size, :]).astype(BF16)
 
-    run(plan.step(0, 3))
-    run(plan.step(0, 4))
+    run(plan.step(0, 2))
     run(plan.step(1, 1))
 
     def layer_norm(z, gain, shift):
@@ -266,6 +251,7 @@
                 wa_ref[j, h * HEAD_DIM:(h + 1) * HEAD_DIM, :] = mixed[j * HEAD_DIM:(j + 1) * HEAD_DIM]
 
     scale = HEAD_DIM ** -0.25
+    half = TILE // 2
     eye_k = eye(TILE // 2)
 
     def pre(t):
@@ -274,10 +260,9 @@
         a = a_ref[t]
         q = (mm(wa_ref[0], a) * scale).astype(BF16)
         for h in range(heads):
-            half = HEAD_DIM * (h % 2)
-            q_ref[h, t, half:half + HEAD_DIM, :] = q[h * HEAD_DIM:(h + 1) * HEAD_DIM]
+            lo = HEAD_DIM * (h % 2)
+            q_ref[h, t, lo:lo + HEAD_DIM, :] = q[h * HEAD_DIM:(h + 1) * HEAD_DIM]
         kt = (mm(wa_ref[1], a) * scale).astype(BF16)
-        half = TILE // 2
         for b in range(2):
             kn = mm_nt(eye_k, kt[:, b * half:(b + 1) * half]).astype(BF16)
             for p in range(pairs):
@@ -339,6 +324,18 @@
         y = r.astype(F32) + (mm(w2t_ref[...], z_ref[...]) + column(0, model + 2))
         h_ref[t] = y.astype(BF16)
 
+    half = TILE // 2
+
+    def out_copy(t):
+        rows_out = pl.ds(pl.multiple_of(t * TILE, TILE), TILE)
+        return pltpu.make_async_copy(y_ref.at[rows_out, :], out_hbm.at[rows_out, :], out_sem.at[t])
+
+    def write_out(t):
+        for b in range(2):
+            y = mm_nt(eye_k, h_ref[t, :, b * half:(b + 1) * half]).astype(BF16)
+            y_ref[pl.ds(pl.multiple_of(t * TILE + b * half, half), half), :] = y
+        out_copy(t).start()
+
     for layer in range(layers):
         more = layer + 1 < layers
         if layer == 0:
@@ -347,24 +344,25 @@
         lax.fori_loop(0, tiles, lambda t, c: (pre(t), c)[1], 0)
         events = {}
         if layer == 0:
-            run(plan.step(1, 2))
-            events[0, 3] = plan.step(1, 3)
-            events[1, 0] = plan.step(1, 4)
+            events[0, 3] = plan.step(1, 2)
         if more:
-            events.setdefault((1, 0), []).extend(plan.step(layer + 2, 1))
-            events[1, 3] = plan.step(layer + 2, 2)
-            events[2, 0] = (plan.hand_over(1, everything=True) if layer == 0 else []) + plan.step(layer + 2, 3)
-            events[2, 3] = plan.step(layer + 2, 4)
+            events.setdefault((0, 3), []).extend(plan.step(layer + 2, 1))
+            if layer == 0:
+                events[2, 0] = plan.hand_over(1, everything=True)
+            events[2, 3] = plan.step(layer + 2, 2)
         attention(events)
         if layer == 0:
             finish(1)
         unpack_mlp(layer)
+        finals = not more
         late = plan.hand_over(layer + 2, everything=True) if more else []
 
         def tile(t, carry, layer=layer, late=late):
             if late:
                 pl.when(t == 1)(functools.partial(run, late))
             post(layer, t)
+            if finals:
+                write_out(t)
             return carry
 
         lax.fori_loop(0, tiles, tile, 0)
@@ -372,11 +370,7 @@
             finish(layer + 2)
 
     for t in range(tiles):
-        for b in range(2):
-            lo = t * TILE + b * (TILE // 2)
-            size = min(TILE // 2, frames - lo)
-            y = mm_nt(eye_k, h_ref[t, :, b * (TILE // 2):(b + 1) * (TILE // 2)]).astype(BF16)
-            out_ref[0, lo:lo + size, :] = y[0:size]
+        out_copy(t).wait()
 
     for piece in range(len(pieces)):
         for m in range(len(MESSAGES)):
@@ -395,7 +389,7 @@
         hidden = hidden_cols * n
         aug = model + LANES
         rows = four * cols
-        attn = jnp.transpose(attn_w, (0, 3, 1, 2)).reshape(layers, rows, model)
+        attn = jnp.transpose(attn_w, (0, 3, 1, 2))
         fc1 = jnp.transpose(fc1_w, (0, 2, 1))
 
         tiles = -(-frames // TILE)
@@ -404,17 +398,19 @@
         heads = model // HEAD_DIM
         pieces = layers + 1
         vmem = pl.BlockSpec(memory_space=pltpu.VMEM)
-        return pl.pallas_call(
+        out = pl.pallas_call(
             functools.partial(kernel, n),
-            out_shape=jax.ShapeDtypeStruct(audio_x.shape, audio_x.dtype),
+            out_shape=jax.ShapeDtypeStruct((padded, model), audio_x.dtype),
             in_specs=[pl.BlockSpec(memory_space=pl.ANY)] + [vmem] * 5,
-            out_specs=vmem,
+            out_specs=pl.BlockSpec(memory_space=pl.ANY),
             scratch_shapes=[
                 pltpu.VMEM((layers, rows, 2 * aug + model), BF16),
+                pltpu.VMEM((rows, model), F32),
                 pltpu.VMEM((layers, n * rows, 2 * aug + model), BF16),
                 pltpu.VMEM((four, model, aug), BF16),
                 pltpu.VMEM((model, hidden), BF16),
                 pltpu.VMEM((frames, model), BF16),
+                pltpu.VMEM((padded, model), BF16),
                 pltpu.VMEM((tiles, model, TILE), BF16),
                 pltpu.VMEM((tiles, aug, TILE), BF16),
                 pltpu.VMEM((heads, tiles, LANES, TILE), BF16),
@@ -427,6 +423,7 @@
                 pltpu.VMEM((1, TILE), F32),
                 pltpu.VMEM((1, TILE), F32),
                 pltpu.SemaphoreType.DMA,
+                pltpu.SemaphoreType.DMA((tiles,)),
                 pltpu.SemaphoreType.DMA((pieces, len(MESSAGES))),
                 pltpu.SemaphoreType.DMA((pieces, len(MESSAGES))),
                 pltpu.SemaphoreType.DMA((pieces, len(BLOCKS) + 1)),
@@ -435,6 +432,7 @@
             compiler_params=pltpu.CompilerParams(
                 collective_id=0, has_side_effects=True, vmem_limit_bytes=60 * 1024 * 1024),
         )(audio_x, attn, fc1, fc2_w, vec_d, b1_vec)
+        return out[None, :frames]
 
     return jax.shard_map(
         body, mesh=mesh,

time: 98.7 us -> 93.8 us (0.950)
  Pallas kernels: 94.3 us -> 91.2 us
  local copies, waits for them, and re-layouts: 3.92 us -> 2.38 us
    pallas_call x1, Pallas kernels: 94.3 us -> 91.2 us  [body(): pl.pallas_call(functools.partial(kernel, n), out_shape=jax.ShapeDtypeStru...]
    broadcast_in_dim x0 -> x1, local copies, waits for them, and re-layouts: none -> 2.38 us  [body(): return out[None, :frames]]
    unnamed x1 -> x0, local copies, waits for them, and re-layouts: 2.38 us -> none
    reshape x1 -> x0, local copies, waits for them, and re-layouts: 1.54 us -> none  [body(): attn = jnp.transpose(attn_w, (0, 3, 1, 2)).reshape(layers, rows, model)]
where the time goes in v2:
time: 93.8 us; the launch traced here: 93.6 us
  Pallas kernels  91.2 us (97%)
  local copies, waits for them, and re-layouts  2.38 us (3%)
    pallas_call x1, Pallas kernels, body(): pl.pallas_call(functools.partial(kernel, n), out_shape=jax.ShapeDtypeStru...  91.2 us
    broadcast_in_dim x1, local copies, waits for them, and re-layouts, body(): return out[None, :frames]  2.38 us

profile of v2, /device:TPU:97, one launch (start us, length us, event | category | flops | bytes accessed | tf_op | source)
XLA Modules:
  0.0 93.6 jit_solution(173799437220069080)
XLA Ops:
  0.0 91.2 %shard_map.64 = bf16[1536,384]{1,0:T(8,128)(2,1)} custom-call(bf16[1,1500,384]{2,1,0:T(8,128)(2,1)} %x_hbm.1, bf16[2,12,4,384]{3,2,1,0:T(4,128)(2,1)} %bitcast.4, bf16[2,48,384]{2,1,0:T(8,128)(2,1)} %bitcast.5, bf16[2,48,384]{2,1,0:T(8,128)(2,1)} %fc2_ref.1, bf16[2,8,12]{2,1,0:T(8,128)(2,1)} %vec_ref.1, bf16[2,48]{1,0:T(2,128)(2,1)} %b1_ref.1), custom_call_target="tpu_custom_call" | custom-call | tf_op jit(solution)/shard_map/pallas_call | solution.py:401
  91.2 2.4 %slice_bitcast_fusion = bf16[1,1500,384]{2,1,0:T(8,128)(2,1)} fusion(bf16[1536,384]{1,0:T(8,128)(2,1)} %shard_map.64), kind=kLoop, calls=%fused_computation | loop fusion | bytes 2304000 | tf_op jit(solution)/shard_map/broadcast_in_dim | solution.py:435

commit v3 on v2

--- a/solution.py
+++ b/solution.py
@@ -11,6 +11,8 @@
 LN_EPSILON = 1e-5
 LANES = 128
 TILE = 512
+KEY_BLOCK = 256
+LAG = 2
 F32, BF16 = jnp.float32, jnp.bfloat16
 NT = (((1,), (1,)), ((), ()))
 
@@ -74,7 +76,7 @@
             if message[0] == step:
                 actions += self.need(piece, message[-1])
                 actions.append(("start", piece, m))
-        if step == 1:
+        if step == 1 and piece == 0:
             actions.append(("pass", piece, len(BLOCKS)))
         return actions + self.hand_over(piece)
 
@@ -84,6 +86,11 @@
         return actions
 
     def hand_over(self, piece, everything=False):
+        if piece:
+            if not everything or (piece, "all") in self.passed:
+                return []
+            self.passed.add((piece, "all"))
+            return self.need(piece, range(len(MESSAGES))) + [("pass", piece, len(BLOCKS))]
         actions = []
         for b, block in enumerate(BLOCKS):
             if (piece, b) in self.passed:
@@ -99,7 +106,7 @@
 
 
 def kernel(n, x_hbm, attn_ref, fc1_ref, fc2_ref, vec_ref, b1_ref, out_hbm, w_ref, row_ref, g_ref, wa_ref, w2t_ref, x_ref, y_ref, h_ref, a_ref,
-           q_ref, k_ref, v_ref, o_ref, z_ref, s0_ref, s1_ref, m0_ref, m1_ref, x_sem, out_sem, send_sem, recv_sem, fsend_sem, frecv_sem):
+           q_ref, k_ref, v_ref, o_ref, z_ref, s0_ref, s1_ref, m0_ref, m1_ref, acc_ref, x_sem, out_sem, send_sem, recv_sem, fsend_sem, frecv_sem):
     layers, rows, width = w_ref.shape
     _, frames, model = x_hbm.shape
     aug = wa_ref.shape[2]
@@ -166,7 +173,7 @@
 
     pl.semaphore_wait(barrier, len(neighbour) + 1)
 
-    pieces = [(0, 0, aug), (0, aug, width - aug)] + [(layer, 0, width) for layer in range(1, layers)]
+    pieces = [piece for layer in range(layers) for piece in ((layer, 0, aug), (layer, aug, width - aug))]
 
     def lanes_of(piece, part, parts):
         _, lo, size = pieces[piece]
@@ -188,7 +195,9 @@
 
     def hand(piece, b):
         lanes = lanes_of(piece, 0, 1)
-        if b == len(BLOCKS):
+        if piece:
+            src = dst = g_ref.reshape(layers, n // 2, 2, rows, width).at[pieces[piece][0], :, core, :, lanes]
+        elif b == len(BLOCKS):
             src, dst = w_ref.at[pieces[piece][0], :, lanes], slot(piece, me, lanes)
         else:
             src = dst = slot(piece, device(BLOCKS[b]), lanes)
@@ -207,8 +216,11 @@
 
     def finish(piece):
         run(plan.hand_over(piece, everything=True))
-        for b in range(len(BLOCKS) + 1):
+        for b in handed(piece):
             hand(piece, b).wait_recv()
+
+    def handed(piece):
+        return range(len(BLOCKS) + 1) if piece == 0 else [len(BLOCKS)]
 
     plan = Planner()
     run(plan.step(0, 1))
@@ -230,6 +242,8 @@
 
     run(plan.step(0, 2))
     run(plan.step(1, 1))
+    if layers > 1:
+        run(plan.step(2, 1))
 
     def layer_norm(z, gain, shift):
         mean = jnp.sum(z, axis=0, keepdims=True) * (1.0 / model)
@@ -254,77 +268,108 @@
     half = TILE // 2
     eye_k = eye(TILE // 2)
 
-    def pre(t):
-        lanes = pl.ds(pl.multiple_of(t * TILE, TILE), TILE)
-        a_ref[t, 0:model, :] = layer_norm(h_ref[t].astype(F32), column(0, model + 1), column(1, model + 1))
+    def norm(t, which):
+        gain, shift = column(which, model + 1), column(which + 1, model + 1)
+        a_ref[t, 0:model, :] = layer_norm(h_ref[t].astype(F32), gain, shift)
+
+    def project(t):
         a = a_ref[t]
+        kt = (mm(wa_ref[1], a) * scale).astype(BF16)
         q = (mm(wa_ref[0], a) * scale).astype(BF16)
         for h in range(heads):
             lo = HEAD_DIM * (h % 2)
             q_ref[h, t, lo:lo + HEAD_DIM, :] = q[h * HEAD_DIM:(h + 1) * HEAD_DIM]
-        kt = (mm(wa_ref[1], a) * scale).astype(BF16)
+        v = mm(wa_ref[2], a).astype(BF16)
+        for h in range(heads):
+            v_ref[h, 0:HEAD_DIM, t * TILE:(t + 1) * TILE] = v[h * HEAD_DIM:(h + 1) * HEAD_DIM]
         for b in range(2):
             kn = mm_nt(eye_k, kt[:, b * half:(b + 1) * half]).astype(BF16)
             for p in range(pairs):
-                k_ref[p, pl.ds(pl.multiple_of(t * TILE + b * half, half), half), :] = kn[:, p * LANES:(p + 1) * LANES]
-        v = mm(wa_ref[2], a).astype(BF16)
-        for h in range(heads):
-            v_ref[h, 0:HEAD_DIM, lanes] = v[h * HEAD_DIM:(h + 1) * HEAD_DIM]
+                k_ref[p, t * TILE + b * half:t * TILE + (b + 1) * half, :] = kn[:, p * LANES:(p + 1) * LANES]
+
+    def pre():
+        norm(0, 0)
+        for t in range(tiles):
+            if t + 1 < tiles:
+                norm(t + 1, 0)
+            project(t)
 
     s_refs, m_refs = (s0_ref, s1_ref), (m0_ref, m1_ref)
 
-    def scores(p, hh, t, buf):
-        s = mm(k_ref[p, 0:keys, :], q_ref[2 * p + hh, t])
-        last = keys - 8
-        row = lax.broadcasted_iota(jnp.int32, (8, TILE), 0) + last
-        tail = jnp.where(row < frames, s[last:], -jnp.inf)
-        s_refs[buf][0:last, :] = s[0:last]
-        s_refs[buf][last:, :] = tail
-        m_refs[buf][...] = jnp.maximum(jnp.max(s[0:last], axis=0, keepdims=True), jnp.max(tail, axis=0, keepdims=True))
-
-    def values(p, hh, t, buf):
+    blocks = [(lo, min(KEY_BLOCK, keys - lo)) for lo in range(0, keys, KEY_BLOCK)]
+    steps = [(hh, t) for hh in range(2) for t in range(tiles)]
+
+    def scores(p, j, c, top):
+        (hh, t), (lo, size) = steps[j], blocks[c]
+        s_ref = s_refs[j % 2]
+        s = mm(k_ref[p, lo:lo + size, :], q_ref[2 * p + hh, t])
+        whole = size
+        if lo + size > frames:
+            whole = size - 8
+            row = lax.broadcasted_iota(jnp.int32, (8, TILE), 0) + (lo + whole)
+            tail = jnp.where(row < frames, s[whole:], -jnp.inf)
+            s_ref[lo + whole:lo + size, :] = tail
+            top = jnp.maximum(top, tail)
+        s_ref[lo:lo + whole, :] = s[0:whole]
+        high = jnp.max(s[0:whole].reshape(whole // 8, 8, TILE), axis=0)
+        top = high if top is None else jnp.maximum(top, high)
+        if c == len(blocks) - 1:
+            m_refs[j % 2][...] = jnp.max(top, axis=0, keepdims=True)
+        return top
+
+    def values(p, j, c, total):
+        (hh, t), (lo, size) = steps[j], blocks[c]
         h = 2 * p + hh
-        e = jnp.exp(s_refs[buf][...] - m_refs[buf][...]).astype(BF16)
-        o = mm(v_ref[h, :, 0:keys], e)
-        inv = 1.0 / o[HEAD_DIM:HEAD_DIM + 1]
-        o_ref[t, pl.ds(pl.multiple_of(h * HEAD_DIM, HEAD_DIM), HEAD_DIM), :] = (o[0:HEAD_DIM] * inv).astype(BF16)
+        e = jnp.exp(s_refs[j % 2][lo:lo + size, :] - m_refs[j % 2][...]).astype(BF16)
+        part = mm(v_ref[h, :, lo:lo + size], e)
+        total = part if c == 0 else total + part
+        if c == len(blocks) - 1:
+            inv = 1.0 / total[HEAD_DIM:HEAD_DIM + 1]
+            o_ref[t, pl.ds(pl.multiple_of(h * HEAD_DIM, HEAD_DIM), HEAD_DIM), :] = (total[0:HEAD_DIM] * inv).astype(BF16)
+        return total
 
     def attention(events):
-        steps = [(hh, t) for hh in range(2) for t in range(tiles)]
+        count = len(blocks)
 
         def body(p, carry):
-            for j, (hh, t) in enumerate(steps):
+            total = acc_ref[...]
+            for j in range(len(steps)):
                 for (at, when), actions in events.items():
                     if when == j:
                         pl.when(p == at)(functools.partial(run, actions))
-                scores(p, hh, t, j % 2)
-                if j:
-                    values(p, *steps[j - 1], (j - 1) % 2)
-                else:
-                    values(jnp.maximum(p - 1, 0), *steps[-1], 1)
+                top = None
+                for c in range(count):
+                    top = scores(p, j, c, top)
+                    back, at = divmod(j * count + c - LAG - count, count)
+                    if back < 0:
+                        total = values(jnp.maximum(p - 1, 0), back + len(steps), at, total)
+                    else:
+                        total = values(p, back, at, total)
+            acc_ref[...] = total
             return carry
 
         lax.fori_loop(0, pairs, body, 0)
-        values(pairs - 1, *steps[-1], 1)
+        total = acc_ref[...]
+        for k in range(len(steps) * count - LAG - count, len(steps) * count):
+            total = values(pairs - 1, *divmod(k, count), total)
 
     def unpack_mlp(layer):
         for b in range(hidden // TILE):
             w2 = g_ref[layer, b * TILE:(b + 1) * TILE, 2 * aug:2 * aug + model]
             w2t_ref[:, b * TILE:(b + 1) * TILE] = mm_nt(eye_m, w2).astype(BF16)
 
-    def post(layer, t):
+    def out_project(t):
         r = h_ref[t].astype(F32) + mm(wa_ref[3], o_ref[t])
-        r = r.astype(BF16)
-        a_ref[t, 0:model, :] = layer_norm(r.astype(F32), column(2, model + 1), column(3, model + 1))
+        h_ref[t] = r.astype(BF16)
+
+    def mlp(layer, t):
         c = a_ref[t]
         step = 2 * LANES
         for b in range(hidden // step):
             u = mm(g_ref[layer, b * step:(b + 1) * step, aug:2 * aug], c)
             z_ref[b * step:(b + 1) * step, :] = (0.5 * u * (1.0 + lax.erf(u * (2.0 ** -0.5)))).astype(BF16)
-        y = r.astype(F32) + (mm(w2t_ref[...], z_ref[...]) + column(0, model + 2))
+        y = h_ref[t].astype(F32) + (mm(w2t_ref[...], z_ref[...]) + column(0, model + 2))
         h_ref[t] = y.astype(BF16)
-
-    half = TILE // 2
 
     def out_copy(t):
         rows_out = pl.ds(pl.multiple_of(t * TILE, TILE), TILE)
@@ -341,33 +386,37 @@
         if layer == 0:
             finish(0)
         unpack(layer)
-        lax.fori_loop(0, tiles, lambda t, c: (pre(t), c)[1], 0)
-        events = {}
+        pre()
+        this, after = 2 * layer + 1, 2 * layer + 2
+        events = {(0, 0): plan.step(this, 2) if layer == 0 else plan.hand_over(this, everything=True)}
+        if more:
+            if layer:
+                events[0, 0] += plan.step(after, 1)
+            events[0, 3] = plan.step(after, 2) + plan.step(after + 1, 1)
         if layer == 0:
-            events[0, 3] = plan.step(1, 2)
+            events[pairs - 1, 0] = plan.hand_over(this, everything=True)
         if more:
-            events.setdefault((0, 3), []).extend(plan.step(layer + 2, 1))
-            if layer == 0:
-                events[2, 0] = plan.hand_over(1, everything=True)
-            events[2, 3] = plan.step(layer + 2, 2)
+            events[pairs - 1, 3] = plan.hand_over(after, everything=True)
         attention(events)
-        if layer == 0:
-            finish(1)
+        finish(this)
+        if more:
+            run(plan.step(after + 1, 2))
+        out_project(0)
         unpack_mlp(layer)
-        finals = not more
-        late = plan.hand_over(layer + 2, everything=True) if more else []
-
-        def tile(t, carry, layer=layer, late=late):
-            if late:
-                pl.when(t == 1)(functools.partial(run, late))
-            post(layer, t)
-            if finals:
+        for t in range(tiles):
+            if t + 1 < tiles:
+                out_project(t + 1)
+            norm(t, 2)
+
+        def tile(t, carry, layer=layer, more=more):
+            mlp(layer, t)
+            if not more:
                 write_out(t)
             return carry
 
         lax.fori_loop(0, tiles, tile, 0)
         if more:
-            finish(layer + 2)
+            finish(after)
 
     for t in range(tiles):
         out_copy(t).wait()
@@ -375,7 +424,7 @@
     for piece in range(len(pieces)):
         for m in range(len(MESSAGES)):
             relay(piece, m).wait_send()
-        for b in range(len(BLOCKS) + 1):
+        for b in handed(piece):
             hand(piece, b).wait_send()
 
 
@@ -396,7 +445,7 @@
         padded = tiles * TILE
         keys = -(-frames // 16) * 16
         heads = model // HEAD_DIM
-        pieces = layers + 1
+        pieces = 2 * layers
         vmem = pl.BlockSpec(memory_space=pltpu.VMEM)
         out = pl.pallas_call(
             functools.partial(kernel, n),
@@ -422,6 +471,7 @@
                 pltpu.VMEM((keys, TILE), F32),
                 pltpu.VMEM((1, TILE), F32),
                 pltpu.VMEM((1, TILE), F32),
+                pltpu.VMEM((HEAD_DIM + 16, TILE), F32),
                 pltpu.SemaphoreType.DMA,
                 pltpu.SemaphoreType.DMA((tiles,)),
                 pltpu.SemaphoreType.DMA((pieces, len(MESSAGES))),

time: 93.8 us -> 78.2 us (0.83)
  Pallas kernels: 91.2 us -> 75.6 us
    pallas_call x1, Pallas kernels: 91.2 us -> 75.6 us  [body(): pl.pallas_call(functools.partial(kernel, n), out_shape=jax.ShapeDtypeStru...]
where the time goes in v3:
time: 78.2 us; the launch traced here: 78 us
  Pallas kernels  75.6 us (97%)
  local copies, waits for them, and re-layouts  2.38 us (3%)
    pallas_call x1, Pallas kernels, body(): pl.pallas_call(functools.partial(kernel, n), out_shape=jax.ShapeDtypeStru...  75.6 us
    broadcast_in_dim x1, local copies, waits for them, and re-layouts, body(): return out[None, :frames]  2.38 us

profile of v3, /device:TPU:97, one launch (start us, length us, event | category | flops | bytes accessed | tf_op | source)
XLA Modules:
  0.0 78.0 jit_solution(3054384244037981043)
XLA Ops:
  0.0 75.6 %shard_map.64 = bf16[1536,384]{1,0:T(8,128)(2,1)} custom-call(bf16[1,1500,384]{2,1,0:T(8,128)(2,1)} %x_hbm.1, bf16[2,12,4,384]{3,2,1,0:T(4,128)(2,1)} %bitcast.4, bf16[2,48,384]{2,1,0:T(8,128)(2,1)} %bitcast.5, bf16[2,48,384]{2,1,0:T(8,128)(2,1)} %fc2_ref.1, bf16[2,8,12]{2,1,0:T(8,128)(2,1)} %vec_ref.1, bf16[2,48]{1,0:T(2,128)(2,1)} %b1_ref.1), custom_call_target="tpu_custom_call" | custom-call | tf_op jit(solution)/shard_map/pallas_call | solution.py:450
  75.6 2.4 %slice_bitcast_fusion = bf16[1,1500,384]{2,1,0:T(8,128)(2,1)} fusion(bf16[1536,384]{1,0:T(8,128)(2,1)} %shard_map.64), kind=kLoop, calls=%fused_computation | loop fusion | bytes 2304000 | tf_op jit(solution)/shard_map/broadcast_in_dim | solution.py:485

commit v4 on v3

--- a/solution.py
+++ b/solution.py
@@ -105,36 +105,49 @@
         return actions
 
 
-def kernel(n, x_hbm, attn_ref, fc1_ref, fc2_ref, vec_ref, b1_ref, out_hbm, w_ref, row_ref, g_ref, wa_ref, w2t_ref, x_ref, y_ref, h_ref, a_ref,
+def kernel(n, x_hbm, attn_hbm, fc1_hbm, fc2_hbm, vec_hbm, b1_hbm, out_hbm, attn_ref, fc1_ref, fc2_ref, vec_ref, b1_ref, w_ref, row_ref, g_ref, wa_ref, w2t_ref, x_ref, y_ref, h_ref, a_ref,
            q_ref, k_ref, v_ref, o_ref, z_ref, s0_ref, s1_ref, m0_ref, m1_ref, acc_ref, x_sem, out_sem, send_sem, recv_sem, fsend_sem, frecv_sem):
     layers, rows, width = w_ref.shape
     _, frames, model = x_hbm.shape
-    aug = wa_ref.shape[2]
+    aug = wa_ref.shape[3]
     heads = model // HEAD_DIM
     pairs = heads // 2
     hidden = z_ref.shape[0]
     tiles = h_ref.shape[0]
     keys = s0_ref.shape[0]
 
-    fetch_x = pltpu.make_async_copy(x_hbm.at[0], x_ref, x_sem)
-    fetch_x.start()
-
     me = lax.axis_index("dp")
     core = lax.rem(me, 2)
     chip = me // 2
     chip_x, chip_y = lax.rem(chip, RING), chip // RING
 
+    @functools.cache
     def device(offset):
         x = lax.rem(chip_x + offset[0] + RING, RING)
         y = lax.rem(chip_y + offset[1] + RING, RING)
         return 2 * (y * RING + x) + core
 
     partner = me + 1 - 2 * core
-    neighbour = {to: device(to) for step, _, _, to, _ in MESSAGES if step == 1}
+    neighbour = {to: device((to[0] % RING, to[1] % RING)) for step, _, _, to, _ in MESSAGES if step == 1}
+    for offset in BLOCKS + [(0, 0)]:
+        device(offset)
 
     barrier = pltpu.get_barrier_semaphore()
     for dev in [*neighbour.values(), partner]:
         pl.semaphore_signal(barrier, inc=1, device_id={"dp": dev})
+
+    fetches = [pltpu.make_async_copy(src, dst, x_sem.at[i]) for i, (src, dst) in enumerate([
+        (attn_hbm, attn_ref), (vec_hbm, vec_ref), (fc1_hbm, fc1_ref), (fc2_hbm, fc2_ref), (b1_hbm, b1_ref), (x_hbm.at[0], x_ref)])]
+    for fetch in fetches:
+        fetch.start()
+    fetch_x = fetches.pop()
+
+    ones_row = (lax.broadcasted_iota(jnp.int32, (aug - model, TILE), 0) == 0).astype(F32).astype(BF16)
+    for t in range(tiles):
+        a_ref[t, model:, :] = ones_row
+        o_ref[t, model:, :] = ones_row
+    for fetch in fetches:
+        fetch.wait()
 
     def pick(layer, want):
         row = lax.broadcasted_iota(jnp.int32, (rows, vec_ref.shape[1]), 0)
@@ -166,11 +179,6 @@
     own = pl.ds(pl.multiple_of(me * rows, 16), rows)
     for layer in range(layers):
         g_ref[layer, own, :] = w_ref[layer]
-    ones_row = (lax.broadcasted_iota(jnp.int32, (aug - model, TILE), 0) == 0).astype(F32).astype(BF16)
-    for t in range(tiles):
-        a_ref[t, model:, :] = ones_row
-        o_ref[t, model:, :] = ones_row
-
     pl.semaphore_wait(barrier, len(neighbour) + 1)
 
     pieces = [piece for layer in range(layers) for piece in ((layer, 0, aug), (layer, aug, width - aug))]
@@ -251,8 +259,8 @@
         var = jnp.sum(c * c, axis=0, keepdims=True) * (1.0 / model)
         return (c * lax.rsqrt(var + LN_EPSILON) * gain + shift).astype(BF16)
 
-    def column(j, lane):
-        return wa_ref[j, :, lane:lane + 1].astype(F32)
+    def column(layer, j, lane):
+        return wa_ref[layer, j, :, lane:lane + 1].astype(F32)
 
     def unpack(layer):
         block = 4 * HEAD_DIM
@@ -262,37 +270,30 @@
         for h in range(heads):
             mixed = mm(perm, g_ref[layer, h * block:(h + 1) * block, 0:aug]).astype(BF16)
             for j in range(4):
-                wa_ref[j, h * HEAD_DIM:(h + 1) * HEAD_DIM, :] = mixed[j * HEAD_DIM:(j + 1) * HEAD_DIM]
+                wa_ref[layer, j, h * HEAD_DIM:(h + 1) * HEAD_DIM, :] = mixed[j * HEAD_DIM:(j + 1) * HEAD_DIM]
 
     scale = HEAD_DIM ** -0.25
     half = TILE // 2
     eye_k = eye(TILE // 2)
 
-    def norm(t, which):
-        gain, shift = column(which, model + 1), column(which + 1, model + 1)
+    def norm(layer, t, which):
+        gain, shift = column(layer, which, model + 1), column(layer, which + 1, model + 1)
         a_ref[t, 0:model, :] = layer_norm(h_ref[t].astype(F32), gain, shift)
 
-    def project(t):
+    def project(layer, t):
         a = a_ref[t]
-        kt = (mm(wa_ref[1], a) * scale).astype(BF16)
-        q = (mm(wa_ref[0], a) * scale).astype(BF16)
+        kt = (mm(wa_ref[layer, 1], a) * scale).astype(BF16)
+        q = (mm(wa_ref[layer, 0], a) * scale).astype(BF16)
         for h in range(heads):
             lo = HEAD_DIM * (h % 2)
             q_ref[h, t, lo:lo + HEAD_DIM, :] = q[h * HEAD_DIM:(h + 1) * HEAD_DIM]
-        v = mm(wa_ref[2], a).astype(BF16)
+        v = mm(wa_ref[layer, 2], a).astype(BF16)
         for h in range(heads):
             v_ref[h, 0:HEAD_DIM, t * TILE:(t + 1) * TILE] = v[h * HEAD_DIM:(h + 1) * HEAD_DIM]
         for b in range(2):
             kn = mm_nt(eye_k, kt[:, b * half:(b + 1) * half]).astype(BF16)
             for p in range(pairs):
                 k_ref[p, t * TILE + b * half:t * TILE + (b + 1) * half, :] = kn[:, p * LANES:(p + 1) * LANES]
-
-    def pre():
-        norm(0, 0)
-        for t in range(tiles):
-            if t + 1 < tiles:
-                norm(t + 1, 0)
-            project(t)
 
     s_refs, m_refs = (s0_ref, s1_ref), (m0_ref, m1_ref)
 
@@ -314,13 +315,14 @@
         high = jnp.max(s[0:whole].reshape(whole // 8, 8, TILE), axis=0)
         top = high if top is None else jnp.maximum(top, high)
         if c == len(blocks) - 1:
-            m_refs[j % 2][...] = jnp.max(top, axis=0, keepdims=True)
+            m_refs[j % 2][...] = jnp.broadcast_to(jnp.max(top, axis=0, keepdims=True), top.shape)
         return top
 
     def values(p, j, c, total):
         (hh, t), (lo, size) = steps[j], blocks[c]
         h = 2 * p + hh
-        e = jnp.exp(s_refs[j % 2][lo:lo + size, :] - m_refs[j % 2][...]).astype(BF16)
+        s = s_refs[j % 2][lo:lo + size, :].reshape(size // 8, 8, TILE)
+        e = jnp.exp(s - m_refs[j % 2][...][None]).reshape(size, TILE).astype(BF16)
         part = mm(v_ref[h, :, lo:lo + size], e)
         total = part if c == 0 else total + part
         if c == len(blocks) - 1:
@@ -334,8 +336,8 @@
         def body(p, carry):
             total = acc_ref[...]
             for j in range(len(steps)):
-                for (at, when), actions in events.items():
-                    if when == j:
+                for at, actions in events.items():
+                    if j == 0 and actions:
                         pl.when(p == at)(functools.partial(run, actions))
                 top = None
                 for c in range(count):
@@ -358,8 +360,8 @@
             w2 = g_ref[layer, b * TILE:(b + 1) * TILE, 2 * aug:2 * aug + model]
             w2t_ref[:, b * TILE:(b + 1) * TILE] = mm_nt(eye_m, w2).astype(BF16)
 
-    def out_project(t):
-        r = h_ref[t].astype(F32) + mm(wa_ref[3], o_ref[t])
+    def out_project(layer, t):
+        r = h_ref[t].astype(F32) + mm(wa_ref[layer, 3], o_ref[t])
         h_ref[t] = r.astype(BF16)
 
     def mlp(layer, t):
@@ -368,7 +370,7 @@
         for b in range(hidden // step):
             u = mm(g_ref[layer, b * step:(b + 1) * step, aug:2 * aug], c)
             z_ref[b * step:(b + 1) * step, :] = (0.5 * u * (1.0 + lax.erf(u * (2.0 ** -0.5)))).astype(BF16)
-        y = h_ref[t].astype(F32) + (mm(w2t_ref[...], z_ref[...]) + column(0, model + 2))
+        y = h_ref[t].astype(F32) + (mm(w2t_ref[...], z_ref[...]) + column(layer, 0, model + 2))
         h_ref[t] = y.astype(BF16)
 
     def out_copy(t):
@@ -381,42 +383,54 @@
             y_ref[pl.ds(pl.multiple_of(t * TILE + b * half, half), half), :] = y
         out_copy(t).start()
 
+    finish(0)
+    unpack(0)
+    norm(0, 0, 0)
+    for t in range(tiles):
+        if t + 1 < tiles:
+            norm(0, t + 1, 0)
+        project(0, t)
+
     for layer in range(layers):
         more = layer + 1 < layers
+        this, after = 2 * layer + 1, 2 * layer + 2
+        events = {0: [], 1: [], pairs - 1: []}
         if layer == 0:
-            finish(0)
-        unpack(layer)
-        pre()
-        this, after = 2 * layer + 1, 2 * layer + 2
-        events = {(0, 0): plan.step(this, 2) if layer == 0 else plan.hand_over(this, everything=True)}
+            events[0] += plan.step(this, 2)
+        elif more:
+            events[0] += plan.step(after, 1)
         if more:
-            if layer:
-                events[0, 0] += plan.step(after, 1)
-            events[0, 3] = plan.step(after, 2) + plan.step(after + 1, 1)
-        if layer == 0:
-            events[pairs - 1, 0] = plan.hand_over(this, everything=True)
-        if more:
-            events[pairs - 1, 3] = plan.hand_over(after, everything=True)
+            events[1] += plan.step(after, 2) + plan.step(after + 1, 1)
+        events[pairs - 1] += plan.hand_over(this, everything=True)
         attention(events)
         finish(this)
         if more:
+            run(plan.hand_over(after, everything=True))
+        out_project(layer, 0)
+        out_project(layer, 1)
+        norm(layer, 0, 2)
+        out_project(layer, 2)
+        unpack_mlp(layer)
+        norm(layer, 1, 2)
+        mlp(layer, 0)
+        if more:
             run(plan.step(after + 1, 2))
-        out_project(0)
-        unpack_mlp(layer)
-        for t in range(tiles):
-            if t + 1 < tiles:
-                out_project(t + 1)
-            norm(t, 2)
-
-        def tile(t, carry, layer=layer, more=more):
+            finish(after)
+            unpack(layer + 1)
+        else:
+            write_out(0)
+        norm(layer, 2, 2)
+        for t in range(1, tiles):
             mlp(layer, t)
-            if not more:
+            if more:
+                norm(layer + 1, t - 1, 0)
+            else:
                 write_out(t)
-            return carry
-
-        lax.fori_loop(0, tiles, tile, 0)
         if more:
-            finish(after)
+            for t in range(tiles):
+                if t == 1:
+                    norm(layer + 1, tiles - 1, 0)
+                project(layer + 1, t)
 
     for t in range(tiles):
         out_copy(t).wait()
@@ -446,17 +460,21 @@
         keys = -(-frames // 16) * 16
         heads = model // HEAD_DIM
         pieces = 2 * layers
-        vmem = pl.BlockSpec(memory_space=pltpu.VMEM)
         out = pl.pallas_call(
             functools.partial(kernel, n),
             out_shape=jax.ShapeDtypeStruct((padded, model), audio_x.dtype),
-            in_specs=[pl.BlockSpec(memory_space=pl.ANY)] + [vmem] * 5,
+            in_specs=[pl.BlockSpec(memory_space=pl.ANY)] * 6,
             out_specs=pl.BlockSpec(memory_space=pl.ANY),
             scratch_shapes=[
+                pltpu.VMEM(attn.shape, BF16),
+                pltpu.VMEM(fc1.shape, BF16),
+                pltpu.VMEM(fc2_w.shape, BF16),
+                pltpu.VMEM(vec_d.shape, BF16),
+                pltpu.VMEM(b1_vec.shape, BF16),
                 pltpu.VMEM((layers, rows, 2 * aug + model), BF16),
                 pltpu.VMEM((rows, model), F32),
                 pltpu.VMEM((layers, n * rows, 2 * aug + model), BF16),
-                pltpu.VMEM((four, model, aug), BF16),
+                pltpu.VMEM((layers, four, model, aug), BF16),
                 pltpu.VMEM((model, hidden), BF16),
                 pltpu.VMEM((frames, model), BF16),
                 pltpu.VMEM((padded, model), BF16),
@@ -469,10 +487,10 @@
                 pltpu.VMEM((hidden, TILE), BF16),
                 pltpu.VMEM((keys, TILE), F32),
                 pltpu.VMEM((keys, TILE), F32),
-                pltpu.VMEM((1, TILE), F32),
-                pltpu.VMEM((1, TILE), F32),
+                pltpu.VMEM((8, TILE), F32),
+                pltpu.VMEM((8, TILE), F32),
                 pltpu.VMEM((HEAD_DIM + 16, TILE), F32),
-                pltpu.SemaphoreType.DMA,
+                pltpu.SemaphoreType.DMA((6,)),
                 pltpu.SemaphoreType.DMA((tiles,)),
                 pltpu.SemaphoreType.DMA((pieces, len(MESSAGES))),
                 pltpu.SemaphoreType.DMA((pieces, len(MESSAGES))),

time: 78.2 us -> 74.9 us (0.958)
  Pallas kernels: 75.6 us -> 72.4 us
    pallas_call x1, Pallas kernels: 75.6 us -> 72.4 us  [body(): pl.pallas_call(functools.partial(kernel, n), out_shape=jax.ShapeDtypeStru...]
where the time goes in v4:
time: 74.9 us; the launch traced here: 74.8 us
  Pallas kernels  72.4 us (97%)
  local copies, waits for them, and re-layouts  2.38 us (3%)
    pallas_call x1, Pallas kernels, body(): pl.pallas_call(functools.partial(kernel, n), out_shape=jax.ShapeDtypeStru...  72.4 us
    broadcast_in_dim x1, local copies, waits for them, and re-layouts, body(): return out[None, :frames]  2.38 us

profile of v4, /device:TPU:97, one launch (start us, length us, event | category | flops | bytes accessed | tf_op | source)
XLA Modules:
  0.0 74.8 jit_solution(4256855949640323938)
XLA Ops:
  0.0 72.4 %shard_map.64 = bf16[1536,384]{1,0:T(8,128)(2,1)} custom-call(bf16[1,1500,384]{2,1,0:T(8,128)(2,1)} %x_hbm.1, bf16[2,12,4,384]{3,2,1,0:T(4,128)(2,1)} %bitcast.4, bf16[2,48,384]{2,1,0:T(8,128)(2,1)} %bitcast.5, bf16[2,48,384]{2,1,0:T(8,128)(2,1)} %fc2_hbm.1, bf16[2,8,12]{2,1,0:T(8,128)(2,1)} %vec_hbm.1, bf16[2,48]{1,0:T(2,128)(2,1)} %b1_hbm.1), custom_call_target="tpu_custom_call" | custom-call | tf_op jit(solution)/shard_map/pallas_call | solution.py:463
  72.4 2.4 %slice_bitcast_fusion = bf16[1,1500,384]{2,1,0:T(8,128)(2,1)} fusion(bf16[1536,384]{1,0:T(8,128)(2,1)} %shard_map.64), kind=kLoop, calls=%fused_computation | loop fusion | bytes 2304000 | tf_op jit(solution)/shard_map/broadcast_in_dim | solution.py:503

commit v5 on v4

--- a/solution.py
+++ b/solution.py
@@ -278,7 +278,8 @@
 
     def norm(layer, t, which):
         gain, shift = column(layer, which, model + 1), column(layer, which + 1, model + 1)
-        a_ref[t, 0:model, :] = layer_norm(h_ref[t].astype(F32), gain, shift)
+        for lo in range(0, TILE, LANES):
+            a_ref[t, 0:model, lo:lo + LANES] = layer_norm(h_ref[t, :, lo:lo + LANES].astype(F32), gain, shift)
 
     def project(layer, t):
         a = a_ref[t]
@@ -330,7 +331,7 @@
             o_ref[t, pl.ds(pl.multiple_of(h * HEAD_DIM, HEAD_DIM), HEAD_DIM), :] = (total[0:HEAD_DIM] * inv).astype(BF16)
         return total
 
-    def attention(events):
+    def attention(events, before_tail, fillers):
         count = len(blocks)
 
         def body(p, carry):
@@ -351,14 +352,16 @@
             return carry
 
         lax.fori_loop(0, pairs, body, 0)
+        before_tail()
         total = acc_ref[...]
         for k in range(len(steps) * count - LAG - count, len(steps) * count):
             total = values(pairs - 1, *divmod(k, count), total)
-
-    def unpack_mlp(layer):
-        for b in range(hidden // TILE):
-            w2 = g_ref[layer, b * TILE:(b + 1) * TILE, 2 * aug:2 * aug + model]
-            w2t_ref[:, b * TILE:(b + 1) * TILE] = mm_nt(eye_m, w2).astype(BF16)
+            if fillers:
+                fillers.pop(0)()
+
+    def unpack_mlp(layer, b):
+        w2 = g_ref[layer, b * TILE:(b + 1) * TILE, 2 * aug:2 * aug + model]
+        w2t_ref[:, b * TILE:(b + 1) * TILE] = mm_nt(eye_m, w2).astype(BF16)
 
     def out_project(layer, t):
         r = h_ref[t].astype(F32) + mm(wa_ref[layer, 3], o_ref[t])
@@ -402,15 +405,13 @@
         if more:
             events[1] += plan.step(after, 2) + plan.step(after + 1, 1)
         events[pairs - 1] += plan.hand_over(this, everything=True)
-        attention(events)
-        finish(this)
+        fillers = [functools.partial(unpack_mlp, layer, b) for b in range(hidden // TILE)]
+        fillers.insert(2, functools.partial(out_project, layer, 0))
+        fillers += [functools.partial(out_project, layer, 1), functools.partial(norm, layer, 0, 2)]
+        attention(events, functools.partial(finish, this), fillers)
         if more:
             run(plan.hand_over(after, everything=True))
-        out_project(layer, 0)
-        out_project(layer, 1)
-        norm(layer, 0, 2)
         out_project(layer, 2)
-        unpack_mlp(layer)
         norm(layer, 1, 2)
         mlp(layer, 0)
         if more:
@@ -432,14 +433,14 @@
                     norm(layer + 1, tiles - 1, 0)
                 project(layer + 1, t)
 
-    for t in range(tiles):
-        out_copy(t).wait()
-
     for piece in range(len(pieces)):
         for m in range(len(MESSAGES)):
             relay(piece, m).wait_send()
         for b in handed(piece):
             hand(piece, b).wait_send()
+
+    for t in range(tiles):
+        out_copy(t).wait()
 
 
 def solution(mesh):

time: 74.9 us -> 74.6 us (level)
  no operation moved by 1% of the time
where the time goes in v5:
time: 74.6 us; the launch traced here: 74.5 us
  Pallas kernels  72.1 us (97%)
  local copies, waits for them, and re-layouts  2.38 us (3%)
    pallas_call x1, Pallas kernels, body(): pl.pallas_call(functools.partial(kernel, n), out_shape=jax.ShapeDtypeStru...  72.1 us
    broadcast_in_dim x1, local copies, waits for them, and re-layouts, body(): return out[None, :frames]  2.38 us

profile of v5, /device:TPU:97, one launch (start us, length us, event | category | flops | bytes accessed | tf_op | source)
XLA Modules:
  0.0 74.5 jit_solution(7456459098404683864)
XLA Ops:
  0.0 72.1 %shard_map.64 = bf16[1536,384]{1,0:T(8,128)(2,1)} custom-call(bf16[1,1500,384]{2,1,0:T(8,128)(2,1)} %x_hbm.1, bf16[2,12,4,384]{3,2,1,0:T(4,128)(2,1)} %bitcast.4, bf16[2,48,384]{2,1,0:T(8,128)(2,1)} %bitcast.5, bf16[2,48,384]{2,1,0:T(8,128)(2,1)} %fc2_hbm.1, bf16[2,8,12]{2,1,0:T(8,128)(2,1)} %vec_hbm.1, bf16[2,48]{1,0:T(2,128)(2,1)} %b1_hbm.1), custom_call_target="tpu_custom_call" | custom-call | tf_op jit(solution)/shard_map/pallas_call | solution.py:464
  72.1 2.4 %slice_bitcast_fusion = bf16[1,1500,384]{2,1,0:T(8,128)(2,1)} fusion(bf16[1536,384]{1,0:T(8,128)(2,1)} %shard_map.64), kind=kLoop, calls=%fused_computation | loop fusion | bytes 2304000 | tf_op jit(solution)/shard_map/broadcast_in_dim | solution.py:504

commit v6 on v5

--- a/solution.py
+++ b/solution.py
@@ -47,18 +47,18 @@
     both = (1, -1)
     axes = [(1, 0), (-1, 0), (0, 1), (0, -1)]
     corners = [(a, b) for a in both for b in both]
-    own = {to: add(1, (0, 1), at(0, 0), to, ()) for to in axes + corners}
+    own = {to: add(1, (0, 1), at(0, 0), to, ()) for to in corners + axes}
     for (a, b), m in own.items():
         complete[at(-a, -b)] = (m,)
-    for part, s in enumerate(both):
-        for r in (0, 1, -1):
+    for part, (a, b) in enumerate(corners):
+        m = add(2, (part, 4), at(-a, -b), (a, b), (own[a, b],))
+        complete[at(2, 2)] = complete.get(at(2, 2), ()) + (m,)
+    for r in (1, -1, 0):
+        for part, s in enumerate(both):
             m = add(2, (part, 2), at(-s, -r), (s, 0), (own[s, r],))
             complete[at(2, -r)] = complete.get(at(2, -r), ()) + (m,)
             m = add(2, (part, 2), at(-r, -s), (0, s), (own[r, s],))
             complete[at(-r, 2)] = complete.get(at(-r, 2), ()) + (m,)
-    for part, (a, b) in enumerate(corners):
-        m = add(2, (part, 4), at(-a, -b), (a, b), (own[a, b],))
-        complete[at(2, 2)] = complete.get(at(2, 2), ()) + (m,)
     return messages, complete
 
 
@@ -105,7 +105,7 @@
         return actions
 
 
-def kernel(n, x_hbm, attn_hbm, fc1_hbm, fc2_hbm, vec_hbm, b1_hbm, out_hbm, attn_ref, fc1_ref, fc2_ref, vec_ref, b1_ref, w_ref, row_ref, g_ref, wa_ref, w2t_ref, x_ref, y_ref, h_ref, a_ref,
+def kernel(n, x_hbm, attn_hbm, fc1_hbm, fc2_hbm, vec_hbm, b1_hbm, out_hbm, attn_ref, fc1_ref, fc2_ref, vec_ref, b1_ref, w_ref, row_ref, g_ref, wa_ref, w2t_ref, x_ref, y_ref, xhat_ref, h_ref, a_ref,
            q_ref, k_ref, v_ref, o_ref, z_ref, s0_ref, s1_ref, m0_ref, m1_ref, acc_ref, x_sem, out_sem, send_sem, recv_sem, fsend_sem, frecv_sem):
     layers, rows, width = w_ref.shape
     _, frames, model = x_hbm.shape
@@ -248,16 +248,20 @@
         size = min(TILE, frames - t * TILE)
         h_ref[t, :, 0:size] = mm_nt(eye_m, x_ref[t * TILE:t * TILE + size, :]).astype(BF16)
 
+    def normalise(z):
+        mean = jnp.sum(z, axis=0, keepdims=True) * (1.0 / model)
+        c = z - mean
+        var = jnp.sum(c * c, axis=0, keepdims=True) * (1.0 / model)
+        return c * lax.rsqrt(var + LN_EPSILON)
+
+    for t in range(tiles):
+        for lo in range(0, TILE, LANES):
+            xhat_ref[t, :, lo:lo + LANES] = normalise(h_ref[t, :, lo:lo + LANES].astype(F32))
+
     run(plan.step(0, 2))
     run(plan.step(1, 1))
     if layers > 1:
         run(plan.step(2, 1))
-
-    def layer_norm(z, gain, shift):
-        mean = jnp.sum(z, axis=0, keepdims=True) * (1.0 / model)
-        c = z - mean
-        var = jnp.sum(c * c, axis=0, keepdims=True) * (1.0 / model)
-        return (c * lax.rsqrt(var + LN_EPSILON) * gain + shift).astype(BF16)
 
     def column(layer, j, lane):
         return wa_ref[layer, j, :, lane:lane + 1].astype(F32)
@@ -279,7 +283,9 @@
     def norm(layer, t, which):
         gain, shift = column(layer, which, model + 1), column(layer, which + 1, model + 1)
         for lo in range(0, TILE, LANES):
-            a_ref[t, 0:model, lo:lo + LANES] = layer_norm(h_ref[t, :, lo:lo + LANES].astype(F32), gain, shift)
+            lanes = slice(lo, lo + LANES)
+            hat = xhat_ref[t, :, lanes] if (layer, which) == (0, 0) else normalise(h_ref[t, :, lanes].astype(F32))
+            a_ref[t, 0:model, lanes] = (hat * gain + shift).astype(BF16)
 
     def project(layer, t):
         a = a_ref[t]
@@ -479,6 +485,7 @@
                 pltpu.VMEM((model, hidden), BF16),
                 pltpu.VMEM((frames, model), BF16),
                 pltpu.VMEM((padded, model), BF16),
+                pltpu.VMEM((tiles, model, TILE), F32),
                 pltpu.VMEM((tiles, model, TILE), BF16),
                 pltpu.VMEM((tiles, aug, TILE), BF16),
                 pltpu.VMEM((heads, tiles, LANES, TILE), BF16),

time: 74.6 us -> 74.1 us (level)
  Pallas kernels: 72.1 us -> 71.3 us
    pallas_call x1, Pallas kernels: 72.1 us -> 71.3 us  [body(): pl.pallas_call(functools.partial(kernel, n), out_shape=jax.ShapeDtypeStru...]
where the time goes in v6:
time: 74.1 us; the launch traced here: 73.7 us
  Pallas kernels  71.3 us (96%)
  local copies, waits for them, and re-layouts  2.38 us (3%)
    pallas_call x1, Pallas kernels, body(): pl.pallas_call(functools.partial(kernel, n), out_shape=jax.ShapeDtypeStru...  71.3 us
    broadcast_in_dim x1, local copies, waits for them, and re-layouts, body(): return out[None, :frames]  2.38 us

profile of v6, /device:TPU:97, one launch (start us, length us, event | category | flops | bytes accessed | tf_op | source)
XLA Modules:
  0.0 73.7 jit_solution(16211916774256139582)
XLA Ops:
  0.0 71.3 %shard_map.64 = bf16[1536,384]{1,0:T(8,128)(2,1)} custom-call(bf16[1,1500,384]{2,1,0:T(8,128)(2,1)} %x_hbm.1, bf16[2,12,4,384]{3,2,1,0:T(4,128)(2,1)} %bitcast.4, bf16[2,48,384]{2,1,0:T(8,128)(2,1)} %bitcast.5, bf16[2,48,384]{2,1,0:T(8,128)(2,1)} %fc2_hbm.1, bf16[2,8,12]{2,1,0:T(8,128)(2,1)} %vec_hbm.1, bf16[2,48]{1,0:T(2,128)(2,1)} %b1_hbm.1), custom_call_target="tpu_custom_call" | custom-call | tf_op jit(solution)/shard_map/pallas_call | solution.py:470
  71.3 2.4 %slice_bitcast_fusion = bf16[1,1500,384]{2,1,0:T(8,128)(2,1)} fusion(bf16[1536,384]{1,0:T(8,128)(2,1)} %shard_map.64), kind=kLoop, calls=%fused_computation | loop fusion | bytes 2304000 | tf_op jit(solution)/shard_map/broadcast_in_dim | solution.py:511
